TPU v7x, 32 devices: a whole 2x2x4 slice. The times are simulated.
32 devices in a mesh: rep: 2 (over x), px: 4 (over y, core), py: 4 (over z).
Axes of the slice: x: 2, y: 2, z: 4, core: 2. Of those that a mesh axis runs over, the one named last changes fastest.
Arguments:
- density: float32 [4, 128, 128, 128], P('rep', 'px', 'py'), parts along dimension 0, may hold values from -6 to 6
- kernel_factors: float32 [3, 89, 256], replicated, as said below
Outputs:
- potential: float32 [4, 128, 128, 128], P('rep', 'px', 'py'), parts along dimension 0
There are 2 independent parts, one for each index of `rep`. A program takes and returns all parts, laid end to end along the dimension named above; an argument that names none is the same for every part. Nothing has to cross between parts.
Inputs may be any that keep to these rules, and one draw needn't show every extreme that they name: Each factor is even in its frequency, kernel_factors[d, g, k] = kernel_factors[d, g, 256 - k], and is zero at k = 128.
All inputs are finite; a program needn't handle non-finite values.
Results may differ from a plain program's by a relative error of at most 0.00005.
Values sent between devices are 32-bit elements; how exact they have to be, the bound alone decides.
A program may use at most 128 MiB of HBM per device.

v0:
```python
import math

import jax
import jax.numpy as jnp
import numpy as np
from jax import lax
from jax.experimental import pallas as pl
from jax.experimental.pallas import tpu as pltpu
from jax.sharding import PartitionSpec as P

HIGHEST = lax.Precision.HIGHEST
BLOCK = 8


def spectral_table(length, chunks):
    freq = np.arange(length).reshape(chunks, 1, length // chunks, 1)
    angle = (freq * np.arange(length) % (2 * length)) * (math.pi / length)
    both = np.concatenate([np.cos(angle), np.sin(angle)], 1)
    return both.reshape(2 * length, length).astype(np.float32)


def dot(spec, left, right):
    return jnp.einsum(spec, left, right, precision=HIGHEST, preferred_element_type=jnp.float32)


def kernel_block(factors, y_start, y_count, z_start, z_count):
    length = factors.shape[2] // 2
    weights = np.full((length,), 1.0 / length, np.float32)
    weights[0] = 0.5 / length
    factors = factors[:, :, :length] * weights
    factor_y = lax.dynamic_slice_in_dim(factors[1], y_start, y_count, 1)
    factor_z = lax.dynamic_slice_in_dim(factors[2], z_start, z_count, 1)
    pair = factor_z[:, :, None] * factor_y[:, None, :]
    return jnp.einsum("gzy,gx->zyx", pair, factors[0], precision=lax.Precision.HIGHEST)


def plain_body(density, kernel_factors):
    replicas, rows_x, rows_y, length = density.shape
    count_px = lax.axis_size("px")
    count_py = lax.axis_size("py")
    half = count_px // replicas
    trade = [[i + half * r for r in range(replicas)] for i in range(half)]
    lines = [[r * half + i for i in range(half)] for r in range(replicas)]
    index_x = lax.axis_index("px") % half
    index_y = lax.axis_index("py")
    table_z = spectral_table(length, count_py)
    table_y = spectral_table(length, half)
    order = np.arange(length).reshape(replicas, half, rows_x).transpose(1, 0, 2).reshape(-1)
    table_x = spectral_table(length, 1)[:, order]

    held = lax.all_to_all(density, "px", 0, 0, axis_index_groups=trade, tiled=True)
    held = held.reshape(replicas * rows_x, rows_y, length)
    held = dot("kz,xyz->kyx", table_z, held)
    held = lax.all_to_all(held, "py", 0, 1, tiled=True)
    held = dot("qy,kyx->kqx", table_y, held)
    held = lax.all_to_all(held, "px", 1, 2, axis_index_groups=lines, tiled=True)
    z_freq, y_freq = length // count_py, length // half
    kernel = kernel_block(kernel_factors, index_x * y_freq, y_freq, index_y * z_freq, z_freq)
    held = dot("kqx,px->kqp", held, table_x)
    held = held.reshape(2, z_freq, 2, y_freq, 2, length) * kernel[None, :, None, :, None, :]
    held = held.reshape(2 * z_freq, 2 * y_freq, 2 * length)
    held = dot("kqp,px->kqx", held, table_x)
    held = lax.all_to_all(held, "px", 2, 1, axis_index_groups=lines, tiled=True)
    held = dot("kqx,qy->kyx", held, table_y)
    held = lax.all_to_all(held, "py", 1, 0, tiled=True)
    held = dot("kyx,kz->xyz", held, table_z)
    held = held.reshape(replicas, rows_x, rows_y, length)
    return lax.all_to_all(held, "px", 0, 0, axis_index_groups=trade, tiled=True)


def split(values, axis, third_low=False):
    high = values.astype(jnp.bfloat16)
    low = (values - high.astype(jnp.float32)).astype(jnp.bfloat16)
    return jnp.concatenate([high, high, low] if third_low else [high, low, high], axis)


def matmul(left, right, contract=((1,), (0,))):
    return lax.dot_general(left, right, (contract, ((), ())), preferred_element_type=jnp.float32)


def solve_kernel(
    dens, factors, fwd_z, fwd_y, fwd_x, inv_x, inv_y, inv_z, out,
    traded, a_send, a_held, b_send, b_held, g_send, g_held, h_send, h_held, o_send, o_held,
    sems_t, sems_z, sems_x, sems_xi, sems_zi, sems_ti,
):
    replicas, rows_x, rows_y, length = dens.shape
    count_py = lax.axis_size("py")
    half = lax.axis_size("px") // replicas
    me_px, me_py = lax.axis_index("px"), lax.axis_index("py")
    mine, line = lax.div(me_px, half), lax.rem(me_px, half)
    lanes = 2 * length // half
    mid = lanes // 2
    freq_z, freq_y = length // count_py, length // half
    blocks_y, blocks_f = rows_y // BLOCK, freq_z // BLOCK
    started = []

    def send(src, dst, sems, slot, device):
        copy = pltpu.make_async_remote_copy(
            src_ref=src, dst_ref=dst, send_sem=sems.at[(0,) + slot], recv_sem=sems.at[(1,) + slot],
            device_id=device, device_id_type=pl.DeviceIdType.MESH,
        )
        copy.start()
        started.append(copy)
        return copy

    trades = []
    for block in range(blocks_y):
        rows = pl.ds(block * BLOCK, BLOCK)
        for step in range(1, replicas):
            other = lax.rem(mine + step, replicas)
            trades.append(
                send(dens.at[other, :, rows, :], traded.at[mine, :, rows, :], sems_t,
                     (step, block), {"px": line + half * other})
            )
    traded[mine] = dens[mine]
    traded_rows = traded.reshape(replicas * rows_x * rows_y, length)
    a_rows = a_send.reshape(length * rows_y, lanes)

    first = blocks_y // 4
    peers = (2, 1, 3) if count_py == 4 else range(1, count_py)
    arrivals_y = [[] for _ in range(blocks_f)]

    def send_planes(freq, rows, there, slot):
        for step in peers:
            other = lax.rem(me_py + step, count_py)
            theirs = pl.ds(other * freq_z + freq.start, freq.size)
            arrivals_y[freq.start // BLOCK].append(
                send(a_send.at[theirs, rows, :], a_held.at[freq, there, :], sems_z,
                     (step, slot), {"py": other})
            )
        ours = pl.ds(me_py * freq_z + freq.start, freq.size)
        a_held[freq, there, :] = a_send[ours, rows, :]

    for block in range(blocks_y):
        for copy in trades[block * (replicas - 1) : (block + 1) * (replicas - 1)]:
            copy.wait_recv()

        @pl.loop(0, BLOCK, unroll=4)
        def _(step, block=block):
            y = block * BLOCK + step
            cells = traded_rows[pl.ds(y, replicas * rows_x, stride=rows_y), :]
            waves = matmul(fwd_z[...], split(cells, 1), ((1,), (1,)))
            both = jnp.concatenate([waves[:length], waves[length:]], 1)
            a_rows[pl.ds(y, length, stride=rows_y), :] = both

        if block < first:
            rows = pl.ds(block * BLOCK, BLOCK)
            there = pl.ds(pl.multiple_of(me_py * rows_y + block * BLOCK, BLOCK), BLOCK)
            send_planes(pl.ds(0, freq_z), rows, there, block)
    count = rows_y - first * BLOCK
    for block in range(blocks_f):
        rows = pl.ds(first * BLOCK, count)
        there = pl.ds(pl.multiple_of(me_py * rows_y + first * BLOCK, BLOCK), count)
        send_planes(pl.ds(block * BLOCK, BLOCK), rows, there, first + block)

    arrivals = []

    def start_lines(block):
        for copy in arrivals_y[block]:
            copy.wait_recv()

        @pl.loop(block * BLOCK, (block + 1) * BLOCK, unroll=4)
        def _(f):
            waves = matmul(fwd_y[...], split(a_held[f], 0))
            for part in range(half):
                b_send[part, f] = waves[part * 2 * freq_y : (part + 1) * 2 * freq_y]
            b_held[line, f] = b_send[line, f]

        some = pl.ds(block * BLOCK, BLOCK)
        here = []
        for step in range(1, half):
            other = lax.rem(line + step, half)
            here.append(
                send(b_send.at[other, some], b_held.at[line, some], sems_x, (step, block),
                     {"px": mine * half + other})
            )
        arrivals.append(here)

    factor_y = factors[1, pl.ds(pl.multiple_of(line * freq_y, BLOCK), freq_y), :]
    returns = []
    arrivals_z = [[] for _ in range(blocks_y)]

    def finish_lines(block):
        for copy in returns[block]:
            copy.wait_recv()

        @pl.loop(block * BLOCK, (block + 1) * BLOCK, unroll=4)
        def _(f):
            waves = jnp.concatenate([g_held[part, f] for part in range(half)], 0)
            h_send[f] = matmul(inv_y[...], split(waves, 0))
            own = pl.ds(pl.multiple_of(me_py * rows_y, BLOCK), rows_y)
            h_held[me_py * freq_z + f] = h_send[f, own, :]

        some = pl.ds(block * BLOCK, BLOCK)
        there = pl.ds(me_py * freq_z + block * BLOCK, BLOCK)
        last = block == blocks_f - 1
        size = BLOCK if last else rows_y
        for cut in range(rows_y // size):
            for step in peers:
                other = lax.rem(me_py + step, count_py)
                cells = pl.ds(pl.multiple_of(other * rows_y + cut * size, BLOCK), size)
                copy = send(
                    h_send.at[some, cells, :], h_held.at[there, pl.ds(cut * size, size), :],
                    sems_zi, (step, block + cut), {"py": other},
                )
                arrivals_z[cut].append(copy)

    def solve_lines(block):
        for copy in arrivals[block]:
            copy.wait_recv()

        @pl.loop(block * BLOCK, (block + 1) * BLOCK, unroll=4)
        def _(f):
            row = factors[2, pl.ds(me_py * freq_z + f, 1), :]
            kernel = lax.dot_general(
                factor_y * row, factors[0], (((1,), (1,)), ((), ())),
                precision=HIGHEST, preferred_element_type=jnp.float32,
            )
            kernel = jnp.concatenate([kernel, kernel], 1)
            kernel = jnp.concatenate([kernel] * 4, 0)
            ours = [b_held[part, f] for part in range(half)]
            cosines = jnp.concatenate([value[:, :mid] for value in ours], 1)
            sines = jnp.concatenate([value[:, mid:] for value in ours], 1)
            cells = jnp.concatenate([cosines, sines], 0)
            product = matmul(split(cells, 1), fwd_x[...]) * kernel
            cells = matmul(split(product, 1), inv_x[...])
            cosines, sines = cells[: 2 * freq_y], cells[2 * freq_y :]
            for part in range(half):
                cut = slice(part * mid, (part + 1) * mid)
                g_send[part, f] = jnp.concatenate([cosines[:, cut], sines[:, cut]], 1)
            g_held[line, f] = g_send[line, f]

        some = pl.ds(block * BLOCK, BLOCK)
        here = []
        for step in range(1, half):
            other = lax.rem(line + step, half)
            here.append(
                send(g_send.at[other, some], g_held.at[line, some], sems_xi, (step, block),
                     {"px": mine * half + other})
            )
        returns.append(here)

    for stage in range(blocks_f + 2):
        if stage < blocks_f:
            start_lines(stage)
        if 0 <= stage - 1 < blocks_f:
            solve_lines(stage - 1)
        if 0 <= stage - 2:
            finish_lines(stage - 2)

    h_rows = h_held.reshape(length * rows_y, lanes)
    o_rows = o_send.reshape(replicas * rows_x * rows_y, length)
    arrivals = []
    for block in range(blocks_y):
        for copy in arrivals_z[block]:
            copy.wait_recv()

        @pl.loop(block * BLOCK, (block + 1) * BLOCK, unroll=4)
        def _(y):
            waves = h_rows[pl.ds(y, length, stride=rows_y), :].T
            waves = jnp.concatenate([waves[:mid], waves[mid:]], 1)
            cells = matmul(split(waves, 1), inv_z[...])
            o_rows[pl.ds(y, replicas * rows_x, stride=rows_y), :] = cells

        rows = pl.ds(block * BLOCK, BLOCK)
        for step in range(1, replicas):
            other = lax.rem(mine + step, replicas)
            arrivals.append(
                send(o_send.at[other, :, rows, :], o_held.at[mine, :, rows, :], sems_ti,
                     (step, block), {"px": line + half * other})
            )
    out[mine] = o_send[mine]
    for copy in arrivals:
        copy.wait_recv()
    for step in range(1, replicas):
        other = lax.rem(mine + step, replicas)
        out[other] = o_held[other]
    for copy in started:
        copy.wait_send()


def kernel_body(density, kernel_factors):
    replicas, rows_x, rows_y, length = density.shape
    count_py = lax.axis_size("py")
    half = lax.axis_size("px") // replicas
    lanes = 2 * length // half
    freq_z, freq_y = length // count_py, length // half
    weights = np.full((length,), 1.0 / length, np.float32)
    weights[0] = 0.5 / length
    terms = kernel_factors.shape[1]
    factors = (kernel_factors[:, :, :length] * weights).transpose(0, 2, 1)
    factors = jnp.pad(factors, ((0, 0), (0, 0), (0, -terms % 128)))
    order = np.arange(length).reshape(replicas, half, rows_x).transpose(1, 0, 2).reshape(-1)
    table_z = spectral_table(length, 1)
    table_y = spectral_table(length, half)
    table_x = spectral_table(length, 1)[:, order]

    def held(table, axis):
        high = table.astype(jnp.bfloat16)
        low = (table - high.astype(np.float32)).astype(jnp.bfloat16)
        return jnp.asarray(np.concatenate([high, high, low], axis))

    tables = (
        held(table_z, 1), held(table_y, 1), held(table_x.T, 0),
        held(table_x, 0), held(table_y.T, 1), held(table_z, 0),
    )
    f32 = jnp.float32
    lines = (length, rows_y, lanes)
    whole = (freq_z, length, lanes)
    pairs = (half, freq_z, 2 * freq_y, lanes)
    blocks_y, blocks_f = rows_y // BLOCK, freq_z // BLOCK
    dma = pltpu.SemaphoreType.DMA
    return pl.pallas_call(
        solve_kernel,
        out_shape=jax.ShapeDtypeStruct(density.shape, f32),
        in_specs=[pl.BlockSpec(memory_space=pltpu.VMEM)] * 8,
        out_specs=pl.BlockSpec(memory_space=pltpu.VMEM),
        scratch_shapes=[
            pltpu.VMEM(density.shape, f32),
            pltpu.VMEM(lines, f32), pltpu.VMEM(whole, f32),
            pltpu.VMEM(pairs, f32), pltpu.VMEM(pairs, f32),
            pltpu.VMEM(pairs, f32), pltpu.VMEM(pairs, f32),
            pltpu.VMEM(whole, f32), pltpu.VMEM(lines, f32),
            pltpu.VMEM(density.shape, f32), pltpu.VMEM(density.shape, f32),
            dma((2, replicas, blocks_y)), dma((2, count_py, blocks_y // 2 + blocks_f)),
            dma((2, half, blocks_f)), dma((2, half, blocks_f)),
            dma((2, count_py, blocks_f + blocks_y)), dma((2, replicas, blocks_y)),
        ],
        compiler_params=pltpu.CompilerParams(
            has_side_effects=True, vmem_limit_bytes=56 * 2**20
        ),
    )(density, factors, *tables)


def body(density, kernel_factors):
    replicas, _, rows_y, length = density.shape
    lanes = 2 * length * replicas // lax.axis_size("px")
    freq_z = length // lax.axis_size("py")
    if lanes % 128 == 0 and rows_y % BLOCK == 0 and freq_z % BLOCK == 0:
        return kernel_body(density, kernel_factors)
    return plain_body(density, kernel_factors)


def solution(mesh):
    placed = (P("rep", "px", "py", None), P())
    return jax.shard_map(
        body, mesh=mesh, in_specs=placed, out_specs=P("rep", "px", "py", None), check_vma=False
    )
```

profile of v0, /device:TPU:0, one launch (start us, length us, event | category | flops | bytes accessed | tf_op | source)
XLA Modules:
  0.0 125.6 jit_solution(12687722819087067749)
XLA Ops:
  0.0 0.0 slice-start
  0.0 0.9 slice-done
  0.9 0.0 copy-start
  0.9 0.1 copy.11
  1.0 0.5 copy-done
  1.6 0.1 multiply_bitcast_fusion
  1.7 0.7 pad.4.factors
  2.4 121.0 %shard_map.91 = f32[2,32,32,128]{3,2,1,0:T(8,128)} custom-call(f32[2,32,32,128]{3,2,1,0:T(8,128)} %dens.1, f32[3,128,128]{2,1,0:T(8,128)} %pad.4.factors, bf16[256,384]{1,0:T(8,128)(2,1)} %constant.18.clone.fwd_z, bf16[256,384]{1,0:T(8,128)(2,1)} %constant.19.clone.fwd_y, bf16[384,256]{1,0:T(8,128)(2,1)} %constant.20.clone.fwd_x, ...), custom_call_target="tpu_custom_call" | custom-call | tf_op jit(solution)/shard_map/pallas_call | solution.py:313
  123.4 2.3 %copy.13 = f32[2,32,32,128]{3,2,1,0:T(8,128)} copy(f32[2,32,32,128]{3,2,1,0:T(8,128)} %shard_map.91) | data formatting | bytes 2097152
Async XLA Ops:
  0.0 0.9 slice-start
  0.9 0.7 copy-start
where the time goes:
time: 126 us
  Pallas kernels  121 us (96%)
  local copies, waits for them, and re-layouts  4.51 us (4%)
    pallas_call x1, Pallas kernels, kernel_body(): pl.pallas_call(solve_kernel, out_shape=jax.ShapeDtypeStruct(density.shape...  121 us
    unnamed x4, local copies, waits for them, and re-layouts  2.91 us

commit v1 on v0

v1 whole, which is shorter than its diff:
```python
import math

import jax
import jax.numpy as jnp
import numpy as np
from jax import lax
from jax.experimental import pallas as pl
from jax.experimental.pallas import tpu as pltpu
from jax.sharding import PartitionSpec as P

HIGHEST = lax.Precision.HIGHEST
LANES = 128
TILES = 4
PITCH = 136


def spectral_table(length, chunks):
    freq = np.arange(length).reshape(chunks, 1, length // chunks, 1)
    angle = (freq * np.arange(length) % (2 * length)) * (math.pi / length)
    both = np.concatenate([np.cos(angle), np.sin(angle)], 1)
    return both.reshape(2 * length, length).astype(np.float32)


def dot(spec, left, right):
    return jnp.einsum(spec, left, right, precision=HIGHEST, preferred_element_type=jnp.float32)


def kernel_block(factors, y_start, y_count, z_start, z_count):
    length = factors.shape[2] // 2
    weights = np.full((length,), 1.0 / length, np.float32)
    weights[0] = 0.5 / length
    factors = factors[:, :, :length] * weights
    factor_y = lax.dynamic_slice_in_dim(factors[1], y_start, y_count, 1)
    factor_z = lax.dynamic_slice_in_dim(factors[2], z_start, z_count, 1)
    pair = factor_z[:, :, None] * factor_y[:, None, :]
    return jnp.einsum("gzy,gx->zyx", pair, factors[0], precision=lax.Precision.HIGHEST)


def plain_body(density, kernel_factors):
    replicas, rows_x, rows_y, length = density.shape
    count_px = lax.axis_size("px")
    count_py = lax.axis_size("py")
    half = count_px // replicas
    trade = [[i + half * r for r in range(replicas)] for i in range(half)]
    lines = [[r * half + i for i in range(half)] for r in range(replicas)]
    index_x = lax.axis_index("px") % half
    index_y = lax.axis_index("py")
    table_z = spectral_table(length, count_py)
    table_y = spectral_table(length, half)
    order = np.arange(length).reshape(replicas, half, rows_x).transpose(1, 0, 2).reshape(-1)
    table_x = spectral_table(length, 1)[:, order]

    held = lax.all_to_all(density, "px", 0, 0, axis_index_groups=trade, tiled=True)
    held = held.reshape(replicas * rows_x, rows_y, length)
    held = dot("kz,xyz->kyx", table_z, held)
    held = lax.all_to_all(held, "py", 0, 1, tiled=True)
    held = dot("qy,kyx->kqx", table_y, held)
    held = lax.all_to_all(held, "px", 1, 2, axis_index_groups=lines, tiled=True)
    z_freq, y_freq = length // count_py, length // half
    kernel = kernel_block(kernel_factors, index_x * y_freq, y_freq, index_y * z_freq, z_freq)
    held = dot("kqx,px->kqp", held, table_x)
    held = held.reshape(2, z_freq, 2, y_freq, 2, length) * kernel[None, :, None, :, None, :]
    held = held.reshape(2 * z_freq, 2 * y_freq, 2 * length)
    held = dot("kqp,px->kqx", held, table_x)
    held = lax.all_to_all(held, "px", 2, 1, axis_index_groups=lines, tiled=True)
    held = dot("kqx,qy->kyx", held, table_y)
    held = lax.all_to_all(held, "py", 1, 0, tiled=True)
    held = dot("kyx,kz->xyz", held, table_z)
    held = held.reshape(replicas, rows_x, rows_y, length)
    return lax.all_to_all(held, "px", 0, 0, axis_index_groups=trade, tiled=True)


def halves(values):
    high = values.astype(jnp.bfloat16)
    low = (values - high.astype(jnp.float32)).astype(jnp.bfloat16)
    return high, low


def matmul(left, right):
    return lax.dot_general(left, right, (((1,), (0,)), ((), ())), preferred_element_type=jnp.float32)


def sector_kernel(
    dens, factors, fold_z, fold_y, wide, tall, back_tall, back_wide, open_y, open_z, out,
    a, z, b, p, swap, x, e, kern, keep, c_send, c_held, g, g_send, zr, fin,
    flat, turned, gains,
    sems_z, sems_y, sems_c, sems_ci, sems_yi, sems_zi,
):
    replicas, rows_x, rows_y, length = dens.shape
    half = length // 2
    tiles = rows_x // 2
    chunks = tiles // TILES
    me_px, me_py = lax.axis_index("px"), lax.axis_index("py")
    count_px, count_py = lax.axis_size("px"), lax.axis_size("py")
    side, core = lax.div(me_px, 2), lax.rem(me_px, 2)
    sign = 2 * side - 1
    part = side * (me_px - 2) + (1 - side) * (1 - me_px)
    peers = {1: me_py + 1 - 2 * lax.rem(me_py, 2), 2: lax.rem(me_py + 2, count_py), 3: count_py - 1 - me_py}

    def role(py):
        return 1 - lax.div(lax.rem(py + 1, count_py), 2), lax.div(py, 2)

    mine, odd_z = role(me_py)
    outer = mine == 1
    twin = count_px - 1 - me_px
    other = me_px + 1 - 2 * core
    started = []

    def make(src, dst, sems, slot, device):
        return pltpu.make_async_remote_copy(
            src_ref=src, dst_ref=dst, send_sem=sems.at[(0,) + slot], recv_sem=sems.at[(1,) + slot],
            device_id=device, device_id_type=pl.DeviceIdType.MESH,
        )

    def span(chunk):
        return pl.ds(chunk * TILES, TILES)

    def lines(py):
        return pl.ds(pl.multiple_of(py * rows_y, 8), rows_y)

    def row(tile):
        return side * tile + (1 - side) * (rows_x - 1 - tile)

    def fold(replica, chunk):
        left = [dens[replica, row(chunk * TILES + i)] for i in range(TILES)]
        right = [dens[replica, row(tiles + chunk * TILES + i)] for i in range(TILES)]
        both = jnp.concatenate([jnp.concatenate(left, 0), jnp.concatenate(right, 0)], 1)
        waves = matmul(jnp.concatenate(halves(both), 1), fold_z[...])
        for parity in range(2):
            cut = waves[:, parity * length : (parity + 1) * length]
            a[replica, parity, span(chunk)] = cut.reshape(TILES, rows_y, length)

    sends_z = {}
    for chunk in range(chunks):
        for step, peer in peers.items():
            replica, parity = role(peer)
            sends_z[step, chunk] = make(
                a.at[replica, parity, span(chunk)], z.at[span(chunk), lines(me_py), :],
                sems_z, (step, chunk), {"py": peer},
            )
    for replica in range(replicas):
        for chunk in range(chunks):
            fold(replica, chunk)

            @pl.when(outer)
            def _(replica=replica, chunk=chunk):
                for step in ((2, 1) if replica == 0 else (3,)):
                    sends_z[step, chunk].start()

            @pl.when(jnp.logical_not(outer))
            def _(replica=replica, chunk=chunk):
                for step in ((3,) if replica == 0 else (2, 1)):
                    sends_z[step, chunk].start()

    @pl.loop(0, tiles, unroll=4)
    def _(tile):
        z[tile, lines(me_py), :] = a[mine, odd_z, tile]

    terms = factors.shape[1]
    flat[...] = jnp.zeros_like(flat)
    where = lax.broadcasted_iota(jnp.int32, (terms, length), 1)
    weight = jnp.where(where == 0, 0.5 / length, 1.0 / length)
    for dim in range(3):
        flat[dim, 0:terms] = factors[dim, :, 0:length] * weight
    for dim in range(2):
        turned[dim] = flat[dim].T
    high, low = halves(flat[2])
    gains[...] = jnp.concatenate(
        [jnp.concatenate([high, low], 1), jnp.concatenate([high, jnp.zeros_like(low)], 1)], 0
    )

    @pl.loop(0, length, unroll=4)
    def _(f):
        pair = turned[0] * turned[1, pl.ds(f, 1), :]
        sums = matmul(jnp.concatenate(halves(pair), 1), gains[...])
        kern[f] = sums[:, :length] + sums[:, length:]

    sends_y, sends_c = [], []

    def fold_lines(chunk):
        for step in peers:
            sends_z[step, chunk].wait_recv()
        for i in range(0, TILES, 2):
            tile = chunk * TILES + i
            cells = jnp.concatenate([z[tile], z[tile + 1]], 1)
            waves = matmul(fold_y[...], jnp.concatenate(halves(cells), 0))
            for parity in range(2):
                for j in range(2):
                    b[parity, tile + j] = waves[
                        parity * half : (parity + 1) * half, j * length : (j + 1) * length
                    ]
        copy = make(b.at[1 - side, span(chunk)], p.at[span(chunk)], sems_y, (chunk,), {"px": twin})
        copy.start()
        sends_y.append(copy)

    flip = sign.astype(jnp.float32)
    is_odd = core.astype(jnp.float32)
    even_or = (1.0 - is_odd) + is_odd * flip
    odd_or = (1.0 - is_odd) * flip + is_odd

    def fold_sheets(chunk):
        sends_y[chunk].wait_recv()
        for i in range(TILES):
            tile = chunk * TILES + i
            ours, theirs = b[side, tile], p[tile]
            total, gap = ours + theirs, (ours - theirs) * flip
            x[part, tile] = jnp.where(core == 0, total, gap)
            swap[tile] = jnp.where(core == 0, gap, total)
        copy = make(swap.at[span(chunk)], x.at[part, span(chunk)], sems_c, (chunk,), {"px": other})
        copy.start()
        sends_c.append(copy)

    def forward(chunk):
        sends_c[chunk].wait_recv()

        @pl.loop(0, 2)
        def _(where):
            cells = x[where, span(chunk)].reshape(TILES * half, length)
            high, low = halves(cells)
            waves = matmul(jnp.concatenate([high, low, high], 1), wide[odd_z])
            for i in range(TILES):
                high, low = halves(waves[i * half : (i + 1) * half])
                both = matmul(tall[side], jnp.concatenate([high, high, low], 0))
                for j in range(2):
                    start = (where * rows_x + j * tiles + chunk * TILES + i) * PITCH
                    e[pl.ds(pl.multiple_of(start, 8), length), :] = both[:, j * length : (j + 1) * length]

    for stage in range(chunks + 2):
        if stage < chunks:
            fold_lines(stage)
        if 0 <= stage - 1 < chunks:
            fold_sheets(stage - 1)
        if 0 <= stage - 2:
            forward(stage - 2)

    @pl.loop(0, length // 2, unroll=2)
    def _(f):
        cells = jnp.concatenate([e[pl.ds(2 * f + i, half, stride=PITCH), :] for i in range(2)], 1)
        high, low = halves(cells)
        waves = matmul(tall[core], jnp.concatenate([high, high, low], 0))
        product = waves * jnp.concatenate([kern[2 * f], kern[2 * f + 1]], 1)
        cells = matmul(back_tall[core], jnp.concatenate(halves(product), 0))
        cells = cells[:half] + cells[half:]
        for i in range(2):
            e[pl.ds(2 * f + i, half, stride=PITCH), :] = cells[:, i * length : (i + 1) * length]

    sends_ci, sends_yi, sends_zi = [], [], {}

    def backward(chunk):
        for where in (1 - part, part):
            found = []
            for i in range(TILES):
                cells = []
                for j in range(2):
                    start = (where * rows_x + j * tiles + chunk * TILES + i) * PITCH
                    cells.append(e[pl.ds(pl.multiple_of(start, 8), length), :])
                cells = matmul(
                    back_tall[side], jnp.concatenate(halves(jnp.concatenate(cells, 1)), 0)
                )
                found.append(cells[:half] + cells[half:])
            high, low = halves(jnp.concatenate(found, 0))
            cells = matmul(jnp.concatenate([high, low, high], 1), back_wide[odd_z])
            cells = cells.reshape(TILES, half, length)
            if where is part:
                keep[span(chunk)] = cells
            else:
                c_send[span(chunk)] = cells
                copy = make(
                    c_send.at[span(chunk)], c_held.at[span(chunk)], sems_ci, (chunk,), {"px": other}
                )
                copy.start()
                sends_ci.append(copy)

    def open_sheets(chunk):
        sends_ci[chunk].wait_recv()
        for i in range(TILES):
            tile = chunk * TILES + i
            first, second = keep[tile], c_held[tile]
            even = jnp.where(core == 0, first, second)
            odd = jnp.where(core == 0, second, first) * flip
            g[side, tile] = even + odd
            g_send[tile] = even - odd
        copy = make(
            g_send.at[span(chunk)], g.at[side, span(chunk)], sems_yi, (chunk,), {"px": twin}
        )
        copy.start()
        sends_yi.append(copy)

    def open_lines(chunk):
        sends_yi[chunk].wait_recv()
        for i in range(0, TILES, 2):
            tile = chunk * TILES + i
            both = [
                jnp.concatenate([g[parity, tile], g[parity, tile + 1]], 1) for parity in range(2)
            ]
            cells = matmul(open_y[...], jnp.concatenate(halves(jnp.concatenate(both, 0)), 0))
            for j in range(2):
                zr[tile + j] = cells[:, j * length : (j + 1) * length]
        for step in (3, 2, 1):
            copy = make(
                zr.at[span(chunk), lines(peers[step]), :], fin.at[mine, odd_z, span(chunk)],
                sems_zi, (step, chunk), {"py": peers[step]},
            )
            copy.start()
            sends_zi[step, chunk] = copy
        fin[mine, odd_z, span(chunk)] = zr[span(chunk), lines(me_py), :]

    for stage in range(chunks + 2):
        if stage < chunks:
            backward(stage)
        if 0 <= stage - 1 < chunks:
            open_sheets(stage - 1)
        if 0 <= stage - 2:
            open_lines(stage - 2)

    for replica in range(replicas):
        for chunk in range(chunks):

            @pl.when(outer)
            def _(replica=replica, chunk=chunk):
                for step in ((2, 1) if replica == 0 else (3,)):
                    sends_zi[step, chunk].wait_recv()

            @pl.when(jnp.logical_not(outer))
            def _(replica=replica, chunk=chunk):
                for step in ((3,) if replica == 0 else (2, 1)):
                    sends_zi[step, chunk].wait_recv()

            both = [
                fin[replica, parity, span(chunk)].reshape(TILES * rows_y, length) for parity in range(2)
            ]
            cells = matmul(
                jnp.concatenate(halves(jnp.concatenate(both, 1)), 1), open_z[...]
            )
            for i in range(TILES):
                cut = cells[i * rows_y : (i + 1) * rows_y]
                tile = chunk * TILES + i
                out[replica, row(tile)] = cut[:, :length]
                out[replica, row(tiles + tile)] = cut[:, length:]

    for copy in [*sends_z.values(), *sends_y, *sends_c, *sends_ci, *sends_yi, *sends_zi.values()]:
        copy.wait_send()


def twice(table):
    zero = np.zeros_like(table)
    return np.block([[table, zero], [zero, table]])


def tables_of(length):
    half = length // 2
    angle = (np.arange(length)[:, None] * (2 * np.arange(half) + 1) % (4 * length)) * (math.pi / (2 * length))
    waves = np.stack([np.cos(angle), np.sin(angle)]).astype(np.float32)
    high = waves.astype(jnp.bfloat16).astype(np.float32)
    low = waves - high
    near, far = np.eye(half), np.eye(half)[::-1]
    line = np.block([[far, near], [-far, near]])
    sides = [line[:half].T, line[half:].T]
    fold_z = np.concatenate([twice(side) for side in sides], 1)
    fold_z = np.concatenate([fold_z, fold_z], 0)
    fold_y = np.concatenate([line, line], 1)
    open_y = np.concatenate([line.T, line.T], 1)
    open_z = np.concatenate([twice(side.T) for side in sides], 0)
    open_z = np.concatenate([open_z, open_z], 0)
    wide, tall, back_tall, back_wide = [], [], [], []
    for parity in range(2):
        up, down = high[parity], low[parity]
        wide.append(np.concatenate([twice(up.T), twice(up.T), twice(down.T)], 0))
        tall.append(np.concatenate([up, down, up], 1))
        back_tall.append(np.block([[up.T, up.T], [down.T, np.zeros_like(down.T)]]))
        back_wide.append(np.concatenate([twice(up), twice(up), twice(down)], 0))
    found = (fold_z, fold_y, np.stack(wide), np.stack(tall), np.stack(back_tall), np.stack(back_wide), open_y, open_z)
    return [jnp.asarray(table.astype(np.float32).astype(jnp.bfloat16)) for table in found]


def sector_body(density, kernel_factors):
    replicas, rows_x, rows_y, length = density.shape
    half, tiles = length // 2, rows_x // 2
    chunks = tiles // TILES
    count_px, count_py = lax.axis_size("px"), lax.axis_size("py")
    f32, bf16 = jnp.float32, jnp.bfloat16
    dma = pltpu.SemaphoreType.DMA
    sheet = (tiles, half, length)
    return pl.pallas_call(
        sector_kernel,
        out_shape=jax.ShapeDtypeStruct(density.shape, f32),
        in_specs=[pl.BlockSpec(memory_space=pltpu.VMEM)] * 10,
        out_specs=pl.BlockSpec(memory_space=pltpu.VMEM),
        scratch_shapes=[
            pltpu.VMEM((replicas, 2, tiles, rows_y, length), f32),
            pltpu.VMEM((tiles, length, length), f32),
            pltpu.VMEM((2,) + sheet, f32), pltpu.VMEM(sheet, f32), pltpu.VMEM(sheet, f32),
            pltpu.VMEM((2,) + sheet, f32),
            pltpu.VMEM((half * PITCH, length), f32),
            pltpu.VMEM((length, length, length), f32),
            pltpu.VMEM(sheet, f32), pltpu.VMEM(sheet, f32), pltpu.VMEM(sheet, f32),
            pltpu.VMEM((2,) + sheet, f32), pltpu.VMEM(sheet, f32),
            pltpu.VMEM((tiles, length, length), f32),
            pltpu.VMEM((replicas, 2, tiles, rows_y, length), f32),
            pltpu.VMEM((3, length, length), f32), pltpu.VMEM((2, length, length), f32),
            pltpu.VMEM((2 * length, 2 * length), bf16),
            dma((2, count_py, chunks)), dma((2, chunks)), dma((2, chunks)),
            dma((2, chunks)), dma((2, chunks)), dma((2, count_py, chunks)),
        ],
        compiler_params=pltpu.CompilerParams(has_side_effects=True, vmem_limit_bytes=56 * 2**20),
    )(density, kernel_factors, *tables_of(length))


def body(density, kernel_factors):
    replicas, rows_x, rows_y, length = density.shape
    count_px, count_py = lax.axis_size("px"), lax.axis_size("py")
    square = count_px == count_py == 2 * replicas == 4
    whole = rows_x * count_px == rows_y * count_py == length == LANES
    if square and whole and kernel_factors.shape[1] <= LANES:
        return sector_body(density, kernel_factors)
    return plain_body(density, kernel_factors)


def solution(mesh):
    placed = (P("rep", "px", "py", None), P())
    return jax.shard_map(
        body, mesh=mesh, in_specs=placed, out_specs=P("rep", "px", "py", None), check_vma=False
    )
```

time: 126 us -> 87.5 us (0.69)
  Pallas kernels: 121 us -> 85.1 us
  local copies, waits for them, and re-layouts: 4.51 us -> 2.26 us
    pallas_call x1, Pallas kernels: 121 us -> 85.1 us  [sector_body(): pl.pallas_call(sector_kernel, out_shape=jax.ShapeDtypeStruct(density.shap...]
    unnamed x4 -> x1, local copies, waits for them, and re-layouts: 2.91 us -> 2.26 us
where the time goes in v1:
time: 87.5 us; the launch traced here: 87.4 us
  Pallas kernels  85.1 us (97%)
  local copies, waits for them, and re-layouts  2.26 us (3%)
    pallas_call x1, Pallas kernels, sector_body(): pl.pallas_call(sector_kernel, out_shape=jax.ShapeDtypeStruct(density.shap...  85.1 us
    unnamed x1, local copies, waits for them, and re-layouts  2.26 us

profile of v1, /device:TPU:0, one launch (start us, length us, event | category | flops | bytes accessed | tf_op | source)
XLA Modules:
  0.0 87.4 jit_solution(17480794504184451945)
XLA Ops:
  0.0 85.1 %shard_map.100 = f32[2,32,32,128]{3,2,1,0:T(8,128)} custom-call(f32[2,32,32,128]{3,2,1,0:T(8,128)} %dens.1, f32[3,89,256]{2,1,0:T(8,128)} %factors.1, bf16[512,256]{1,0:T(8,128)(2,1)} %constant.16.clone.fold_z, bf16[128,256]{1,0:T(8,128)(2,1)} %constant.17.clone.fold_y, bf16[2,384,256]{2,1,0:T(8,128)(2,1)} %constant.18.clone.wide, ...), custom_call_target="tpu_custom_call" | custom-call | tf_op jit(solution)/shard_map/pallas_call | solution.py:384
  85.1 2.3 %copy.12 = f32[2,32,32,128]{3,2,1,0:T(8,128)} copy(f32[2,32,32,128]{3,2,1,0:T(8,128)} %shard_map.100) | data formatting | bytes 2097152

commit v2 on v1

--- a/solution.py
+++ b/solution.py
@@ -10,7 +10,8 @@
 
 HIGHEST = lax.Precision.HIGHEST
 LANES = 128
-TILES = 4
+TILES = 2
+LAG = 2
 PITCH = 136
 
 
@@ -81,10 +82,11 @@
 
 
 def sector_kernel(
-    dens, factors, fold_z, fold_y, wide, tall, back_tall, back_wide, open_y, open_z, out,
-    a, z, b, p, swap, x, e, kern, keep, c_send, c_held, g, g_send, zr, fin,
+    dens_in, factors_in, fold_z_in, fold_y_in, wide_in, tall_in, back_tall_in, back_wide_in, open_y_in, open_z_in, out,
+    dens, factors, fold_z, fold_y, wide, tall, back_tall, back_wide, open_y, open_z,
+    a, z, b, p, swap, x, e, turned_e, kern, keep, c_send, c_held, g, g_send, zr, fin, found,
     flat, turned, gains,
-    sems_z, sems_y, sems_c, sems_ci, sems_yi, sems_zi,
+    sems_z, sems_y, sems_c, sems_ci, sems_yi, sems_zi, sems_in, sems_out,
 ):
     replicas, rows_x, rows_y, length = dens.shape
     half = length // 2
@@ -98,13 +100,35 @@
     peers = {1: me_py + 1 - 2 * lax.rem(me_py, 2), 2: lax.rem(me_py + 2, count_py), 3: count_py - 1 - me_py}
 
     def role(py):
-        return 1 - lax.div(lax.rem(py + 1, count_py), 2), lax.div(py, 2)
+        return lax.div(lax.rem(py + 1, count_py), 2), lax.div(py, 2)
 
     mine, odd_z = role(me_py)
-    outer = mine == 1
+    outer = mine == 0
     twin = count_px - 1 - me_px
     other = me_px + 1 - 2 * core
-    started = []
+
+    barrier = pltpu.get_barrier_semaphore()
+    partners = [{"py": peer} for peer in peers.values()] + [{"px": twin}, {"px": other}]
+    for partner in partners:
+        pl.semaphore_signal(barrier, inc=1, device_id=partner, device_id_type=pl.DeviceIdType.MESH)
+
+    loads = {}
+
+    def load(name, src, dst):
+        loads[name] = pltpu.make_async_copy(src, dst, sems_in.at[len(loads)])
+        loads[name].start()
+
+    load("first", dens_in.at[0], dens.at[0])
+    load("fold_z", fold_z_in, fold_z)
+    load("rest", dens_in.at[pl.ds(1, replicas - 1)], dens.at[pl.ds(1, replicas - 1)])
+    load("factors", factors_in, factors)
+    load("fold_y", fold_y_in, fold_y)
+    load("wide", wide_in, wide)
+    load("tall", tall_in, tall)
+    load("back_tall", back_tall_in, back_tall)
+    load("back_wide", back_wide_in, back_wide)
+    load("open_y", open_y_in, open_y)
+    load("open_z", open_z_in, open_z)
 
     def make(src, dst, sems, slot, device):
         return pltpu.make_async_remote_copy(
@@ -138,43 +162,59 @@
                 a.at[replica, parity, span(chunk)], z.at[span(chunk), lines(me_py), :],
                 sems_z, (step, chunk), {"py": peer},
             )
+    def steps(replica):
+        return ((3,), (2, 1)) if replica == 0 else ((2, 1), (3,))
+
+    def scatter(replica, chunk):
+        at_outer, at_inner = steps(replica)
+
+        @pl.when(outer)
+        def _():
+            for step in at_outer:
+                sends_z[step, chunk].start()
+
+        @pl.when(jnp.logical_not(outer))
+        def _():
+            for step in at_inner:
+                sends_z[step, chunk].start()
+
+    loads["first"].wait()
+    loads["fold_z"].wait()
     for replica in range(replicas):
+        if replica == 1:
+            loads["rest"].wait()
         for chunk in range(chunks):
             fold(replica, chunk)
-
-            @pl.when(outer)
-            def _(replica=replica, chunk=chunk):
-                for step in ((2, 1) if replica == 0 else (3,)):
-                    sends_z[step, chunk].start()
-
-            @pl.when(jnp.logical_not(outer))
-            def _(replica=replica, chunk=chunk):
-                for step in ((3,) if replica == 0 else (2, 1)):
-                    sends_z[step, chunk].start()
+            if replica == chunk == 0:
+                pl.semaphore_wait(barrier, len(partners))
+            scatter(replica, chunk)
 
     @pl.loop(0, tiles, unroll=4)
     def _(tile):
         z[tile, lines(me_py), :] = a[mine, odd_z, tile]
 
-    terms = factors.shape[1]
-    flat[...] = jnp.zeros_like(flat)
-    where = lax.broadcasted_iota(jnp.int32, (terms, length), 1)
-    weight = jnp.where(where == 0, 0.5 / length, 1.0 / length)
-    for dim in range(3):
-        flat[dim, 0:terms] = factors[dim, :, 0:length] * weight
-    for dim in range(2):
-        turned[dim] = flat[dim].T
-    high, low = halves(flat[2])
-    gains[...] = jnp.concatenate(
-        [jnp.concatenate([high, low], 1), jnp.concatenate([high, jnp.zeros_like(low)], 1)], 0
-    )
-
-    @pl.loop(0, length, unroll=4)
-    def _(f):
-        pair = turned[0] * turned[1, pl.ds(f, 1), :]
-        sums = matmul(jnp.concatenate(halves(pair), 1), gains[...])
-        kern[f] = sums[:, :length] + sums[:, length:]
-
+    def kernel_values():
+        loads["factors"].wait()
+        terms = factors.shape[1]
+        flat[...] = jnp.zeros_like(flat)
+        where = lax.broadcasted_iota(jnp.int32, (terms, length), 1)
+        weight = jnp.where(where == 0, 0.5 / length, 1.0 / length)
+        for dim in range(3):
+            flat[dim, 0:terms] = factors[dim, :, 0:length] * weight
+        for dim in range(2):
+            turned[dim] = flat[dim].T
+        high, low = halves(flat[2])
+        gains[...] = jnp.concatenate(
+            [jnp.concatenate([high, low], 1), jnp.concatenate([high, jnp.zeros_like(low)], 1)], 0
+        )
+
+        @pl.loop(0, length, unroll=8)
+        def _(f):
+            pair = turned[0] * turned[1, pl.ds(f, 1), :]
+            sums = matmul(jnp.concatenate(halves(pair), 1), gains[...])
+            kern[f] = sums[:, :length] + sums[:, length:]
+
+    kernel_values()
     sends_y, sends_c = [], []
 
     def fold_lines(chunk):
@@ -213,8 +253,7 @@
     def forward(chunk):
         sends_c[chunk].wait_recv()
 
-        @pl.loop(0, 2)
-        def _(where):
+        for where in range(2):
             cells = x[where, span(chunk)].reshape(TILES * half, length)
             high, low = halves(cells)
             waves = matmul(jnp.concatenate([high, low, high], 1), wide[odd_z])
@@ -225,25 +264,30 @@
                     start = (where * rows_x + j * tiles + chunk * TILES + i) * PITCH
                     e[pl.ds(pl.multiple_of(start, 8), length), :] = both[:, j * length : (j + 1) * length]
 
-    for stage in range(chunks + 2):
+    for name in ("fold_y", "wide", "tall"):
+        loads[name].wait()
+    for stage in range(chunks + LAG + 1):
         if stage < chunks:
             fold_lines(stage)
-        if 0 <= stage - 1 < chunks:
-            fold_sheets(stage - 1)
-        if 0 <= stage - 2:
-            forward(stage - 2)
-
-    @pl.loop(0, length // 2, unroll=2)
-    def _(f):
-        cells = jnp.concatenate([e[pl.ds(2 * f + i, half, stride=PITCH), :] for i in range(2)], 1)
-        high, low = halves(cells)
-        waves = matmul(tall[core], jnp.concatenate([high, high, low], 0))
-        product = waves * jnp.concatenate([kern[2 * f], kern[2 * f + 1]], 1)
-        cells = matmul(back_tall[core], jnp.concatenate(halves(product), 0))
-        cells = cells[:half] + cells[half:]
-        for i in range(2):
-            e[pl.ds(2 * f + i, half, stride=PITCH), :] = cells[:, i * length : (i + 1) * length]
-
+        if 0 <= stage - LAG < chunks:
+            fold_sheets(stage - LAG)
+        if 0 <= stage - LAG - 1:
+            forward(stage - LAG - 1)
+
+    def middle():
+        @pl.loop(0, length // 2, unroll=4)
+        def _(f):
+            cells = jnp.concatenate([e[pl.ds(2 * f + i, half, stride=PITCH), :] for i in range(2)], 1)
+            high, low = halves(cells)
+            waves = matmul(tall[core], jnp.concatenate([high, high, low], 0))
+            product = waves * jnp.concatenate([kern[2 * f], kern[2 * f + 1]], 1)
+            cells = matmul(back_tall[core], jnp.concatenate(halves(product), 0))
+            cells = cells[:half] + cells[half:]
+            for i in range(2):
+                turned_e[pl.ds(2 * f + i, half, stride=PITCH), :] = cells[:, i * length : (i + 1) * length]
+
+    loads["back_tall"].wait()
+    middle()
     sends_ci, sends_yi, sends_zi = [], [], {}
 
     def backward(chunk):
@@ -253,7 +297,7 @@
                 cells = []
                 for j in range(2):
                     start = (where * rows_x + j * tiles + chunk * TILES + i) * PITCH
-                    cells.append(e[pl.ds(pl.multiple_of(start, 8), length), :])
+                    cells.append(turned_e[pl.ds(pl.multiple_of(start, 8), length), :])
                 cells = matmul(
                     back_tall[side], jnp.concatenate(halves(jnp.concatenate(cells, 1)), 0)
                 )
@@ -296,50 +340,78 @@
             cells = matmul(open_y[...], jnp.concatenate(halves(jnp.concatenate(both, 0)), 0))
             for j in range(2):
                 zr[tile + j] = cells[:, j * length : (j + 1) * length]
-        for step in (3, 2, 1):
-            copy = make(
-                zr.at[span(chunk), lines(peers[step]), :], fin.at[mine, odd_z, span(chunk)],
-                sems_zi, (step, chunk), {"py": peers[step]},
+        for step, peer in peers.items():
+            sends_zi[step, chunk] = make(
+                zr.at[span(chunk), lines(peer), :], fin.at[mine, odd_z, span(chunk)],
+                sems_zi, (step, chunk), {"py": peer},
             )
-            copy.start()
-            sends_zi[step, chunk] = copy
+        for step in (3, 2):
+            sends_zi[step, chunk].start()
+
+        @pl.when(jnp.logical_not(outer))
+        def _():
+            sends_zi[1, chunk].start()
+
         fin[mine, odd_z, span(chunk)] = zr[span(chunk), lines(me_py), :]
 
-    for stage in range(chunks + 2):
+    for name in ("back_wide", "open_y", "open_z"):
+        loads[name].wait()
+    for stage in range(chunks + LAG + 1):
         if stage < chunks:
             backward(stage)
         if 0 <= stage - 1 < chunks:
             open_sheets(stage - 1)
-        if 0 <= stage - 2:
-            open_lines(stage - 2)
+        if 0 <= stage - LAG - 1:
+            open_lines(stage - LAG - 1)
+
+    @pl.when(outer)
+    def _():
+        for chunk in range(chunks):
+            sends_zi[1, chunk].start()
+
+    stores = []
+
+    def finish(replica, chunk):
+        at_outer, at_inner = steps(replica)
+
+        @pl.when(outer)
+        def _():
+            for step in at_outer:
+                sends_zi[step, chunk].wait_recv()
+
+        @pl.when(jnp.logical_not(outer))
+        def _():
+            for step in at_inner:
+                sends_zi[step, chunk].wait_recv()
+
+        both = [
+            fin[replica, parity, span(chunk)].reshape(TILES * rows_y, length) for parity in range(2)
+        ]
+        cells = matmul(
+            jnp.concatenate(halves(jnp.concatenate(both, 1)), 1), open_z[...]
+        )
+        for i in range(TILES):
+            cut = cells[i * rows_y : (i + 1) * rows_y]
+            tile = chunk * TILES + i
+            found[replica, row(tile)] = cut[:, :length]
+            found[replica, row(tiles + tile)] = cut[:, length:]
+        for part_x in range(2):
+            first = part_x * tiles + chunk * TILES
+            rows = pl.ds(side * first + (1 - side) * (rows_x - first - TILES), TILES)
+            copy = pltpu.make_async_copy(
+                found.at[replica, rows], out.at[replica, rows], sems_out.at[replica, chunk, part_x]
+            )
+            copy.start()
+            stores.append(copy)
 
     for replica in range(replicas):
         for chunk in range(chunks):
-
-            @pl.when(outer)
-            def _(replica=replica, chunk=chunk):
-                for step in ((2, 1) if replica == 0 else (3,)):
-                    sends_zi[step, chunk].wait_recv()
-
-            @pl.when(jnp.logical_not(outer))
-            def _(replica=replica, chunk=chunk):
-                for step in ((3,) if replica == 0 else (2, 1)):
-                    sends_zi[step, chunk].wait_recv()
-
-            both = [
-                fin[replica, parity, span(chunk)].reshape(TILES * rows_y, length) for parity in range(2)
-            ]
-            cells = matmul(
-                jnp.concatenate(halves(jnp.concatenate(both, 1)), 1), open_z[...]
-            )
-            for i in range(TILES):
-                cut = cells[i * rows_y : (i + 1) * rows_y]
-                tile = chunk * TILES + i
-                out[replica, row(tile)] = cut[:, :length]
-                out[replica, row(tiles + tile)] = cut[:, length:]
+            finish(replica, chunk)
 
     for copy in [*sends_z.values(), *sends_y, *sends_c, *sends_ci, *sends_yi, *sends_zi.values()]:
         copy.wait_send()
+    for copy in stores:
+        copy.wait()
 
 
 def twice(table):
@@ -381,29 +453,34 @@
     f32, bf16 = jnp.float32, jnp.bfloat16
     dma = pltpu.SemaphoreType.DMA
     sheet = (tiles, half, length)
+    given = (density, kernel_factors, *tables_of(length))
     return pl.pallas_call(
         sector_kernel,
         out_shape=jax.ShapeDtypeStruct(density.shape, f32),
-        in_specs=[pl.BlockSpec(memory_space=pltpu.VMEM)] * 10,
-        out_specs=pl.BlockSpec(memory_space=pltpu.VMEM),
-        scratch_shapes=[
+        in_specs=[pl.BlockSpec(memory_space=pl.ANY)] * len(given),
+        out_specs=pl.BlockSpec(memory_space=pl.ANY),
+        scratch_shapes=[pltpu.VMEM(array.shape, array.dtype) for array in given] + [
             pltpu.VMEM((replicas, 2, tiles, rows_y, length), f32),
             pltpu.VMEM((tiles, length, length), f32),
             pltpu.VMEM((2,) + sheet, f32), pltpu.VMEM(sheet, f32), pltpu.VMEM(sheet, f32),
             pltpu.VMEM((2,) + sheet, f32),
-            pltpu.VMEM((half * PITCH, length), f32),
+            pltpu.VMEM((half * PITCH, length), f32), pltpu.VMEM((half * PITCH, length), f32),
             pltpu.VMEM((length, length, length), f32),
             pltpu.VMEM(sheet, f32), pltpu.VMEM(sheet, f32), pltpu.VMEM(sheet, f32),
             pltpu.VMEM((2,) + sheet, f32), pltpu.VMEM(sheet, f32),
             pltpu.VMEM((tiles, length, length), f32),
             pltpu.VMEM((replicas, 2, tiles, rows_y, length), f32),
+            pltpu.VMEM(density.shape, f32),
             pltpu.VMEM((3, length, length), f32), pltpu.VMEM((2, length, length), f32),
             pltpu.VMEM((2 * length, 2 * length), bf16),
             dma((2, count_py, chunks)), dma((2, chunks)), dma((2, chunks)),
             dma((2, chunks)), dma((2, chunks)), dma((2, count_py, chunks)),
+            dma((len(given) + 1,)), dma((replicas, chunks, 2)),
         ],
-        compiler_params=pltpu.CompilerParams(has_side_effects=True, vmem_limit_bytes=56 * 2**20),
-    )(density, kernel_factors, *tables_of(length))
+        compiler_params=pltpu.CompilerParams(
+            has_side_effects=True, vmem_limit_bytes=56 * 2**20, collective_id=0
+        ),
+    )(*given)
 
 
 def body(density, kernel_factors):

time: 87.5 us -> 73.5 us (0.84)
  Pallas kernels: 85.1 us -> 71 us
    pallas_call x1, Pallas kernels: 85.1 us -> 71 us  [sector_body(): pl.pallas_call(sector_kernel, out_shape=jax.ShapeDtypeStruct(density.shap...]
where the time goes in v2:
time: 73.5 us; the launch traced here: 73.3 us
  Pallas kernels  71 us (97%)
  local copies, waits for them, and re-layouts  2.26 us (3%)
    pallas_call x1, Pallas kernels, sector_body(): pl.pallas_call(sector_kernel, out_shape=jax.ShapeDtypeStruct(density.shap...  71 us
    unnamed x1, local copies, waits for them, and re-layouts  2.26 us

profile of v2, /device:TPU:0, one launch (start us, length us, event | category | flops | bytes accessed | tf_op | source)
XLA Modules:
  0.0 73.3 jit_solution(5698348647499008543)
XLA Ops:
  0.0 71.0 %shard_map.100 = f32[2,32,32,128]{3,2,1,0:T(8,128)} custom-call(f32[2,32,32,128]{3,2,1,0:T(8,128)} %dens_in.1, f32[3,89,256]{2,1,0:T(8,128)} %factors_in.1, bf16[512,256]{1,0:T(8,128)(2,1)} %constant.16.clone.fold_z_in, bf16[128,256]{1,0:T(8,128)(2,1)} %constant.17.clone.fold_y_in, bf16[2,384,256]{2,1,0:T(8,128)(2,1)} %constant.18.clone.wide_in, ...), custom_call_target="tpu_custom_call" | custom-call | tf_op jit(solution)/shard_map/pallas_call | solution.py:457
  71.0 2.3 %copy.12 = f32[2,32,32,128]{3,2,1,0:T(8,128)} copy(f32[2,32,32,128]{3,2,1,0:T(8,128)} %shard_map.100) | data formatting | bytes 2097152

commit v3 on v2

--- a/solution.py
+++ b/solution.py
@@ -11,7 +11,8 @@
 HIGHEST = lax.Precision.HIGHEST
 LANES = 128
 TILES = 2
-LAG = 2
+LAG = 3
+GROUP = 8
 PITCH = 136
 
 
@@ -84,9 +85,9 @@
 def sector_kernel(
     dens_in, factors_in, fold_z_in, fold_y_in, wide_in, tall_in, back_tall_in, back_wide_in, open_y_in, open_z_in, out,
     dens, factors, fold_z, fold_y, wide, tall, back_tall, back_wide, open_y, open_z,
-    a, z, b, p, swap, x, e, turned_e, kern, keep, c_send, c_held, g, g_send, zr, fin, found,
-    flat, turned, gains,
-    sems_z, sems_y, sems_c, sems_ci, sems_yi, sems_zi, sems_in, sems_out,
+    a, z, b, p, swap, x, e, turned_e, kern, keep, c_send, c_held, g, g_send, zr, fin,
+    flat, turned, gains, solved,
+    sems_z, sems_y, sems_c, sems_ci, sems_yi, sems_zi, sems_in,
 ):
     replicas, rows_x, rows_y, length = dens.shape
     half = length // 2
@@ -274,25 +275,42 @@
         if 0 <= stage - LAG - 1:
             forward(stage - LAG - 1)
 
-    def middle():
-        @pl.loop(0, length // 2, unroll=4)
-        def _(f):
-            cells = jnp.concatenate([e[pl.ds(2 * f + i, half, stride=PITCH), :] for i in range(2)], 1)
+    def spectra(f):
+        for k in range(GROUP):
+            first = 2 * (f * GROUP + k)
+            cells = jnp.concatenate([e[pl.ds(first + i, half, stride=PITCH), :] for i in range(2)], 1)
             high, low = halves(cells)
             waves = matmul(tall[core], jnp.concatenate([high, high, low], 0))
-            product = waves * jnp.concatenate([kern[2 * f], kern[2 * f + 1]], 1)
-            cells = matmul(back_tall[core], jnp.concatenate(halves(product), 0))
+            product = waves * jnp.concatenate([kern[first], kern[first + 1]], 1)
+            solved[k] = jnp.concatenate(halves(product), 0)
+
+    def answers(f):
+        for k in range(GROUP):
+            first = 2 * (f * GROUP + k)
+            cells = matmul(back_tall[core], solved[k])
             cells = cells[:half] + cells[half:]
             for i in range(2):
-                turned_e[pl.ds(2 * f + i, half, stride=PITCH), :] = cells[:, i * length : (i + 1) * length]
+                turned_e[pl.ds(first + i, half, stride=PITCH), :] = cells[:, i * length : (i + 1) * length]
+
+    def middle():
+        trips = length // (2 * GROUP)
+        spectra(0)
+
+        @pl.loop(1, trips)
+        def _(f):
+            answers(f - 1)
+            spectra(f)
+
+        answers(trips - 1)
 
     loads["back_tall"].wait()
     middle()
     sends_ci, sends_yi, sends_zi = [], [], {}
 
     def backward(chunk):
+        solved_here = []
         for where in (1 - part, part):
-            found = []
+            rows = []
             for i in range(TILES):
                 cells = []
                 for j in range(2):
@@ -301,19 +319,14 @@
                 cells = matmul(
                     back_tall[side], jnp.concatenate(halves(jnp.concatenate(cells, 1)), 0)
                 )
-                found.append(cells[:half] + cells[half:])
-            high, low = halves(jnp.concatenate(found, 0))
+                rows.append(cells[:half] + cells[half:])
+            high, low = halves(jnp.concatenate(rows, 0))
             cells = matmul(jnp.concatenate([high, low, high], 1), back_wide[odd_z])
-            cells = cells.reshape(TILES, half, length)
-            if where is part:
-                keep[span(chunk)] = cells
-            else:
-                c_send[span(chunk)] = cells
-                copy = make(
-                    c_send.at[span(chunk)], c_held.at[span(chunk)], sems_ci, (chunk,), {"px": other}
-                )
-                copy.start()
-                sends_ci.append(copy)
+            solved_here.append(cells.reshape(TILES, half, length))
+        c_send[span(chunk)], keep[span(chunk)] = solved_here
+        copy = make(c_send.at[span(chunk)], c_held.at[span(chunk)], sems_ci, (chunk,), {"px": other})
+        copy.start()
+        sends_ci.append(copy)
 
     def open_sheets(chunk):
         sends_ci[chunk].wait_recv()
@@ -369,7 +382,8 @@
         for chunk in range(chunks):
             sends_zi[1, chunk].start()
 
-    stores = []
+    for copy in [*sends_z.values(), *sends_y, *sends_c, *sends_ci, *sends_yi]:
+        copy.wait_send()
 
     def finish(replica, chunk):
         at_outer, at_inner = steps(replica)
@@ -393,25 +407,15 @@
         for i in range(TILES):
             cut = cells[i * rows_y : (i + 1) * rows_y]
             tile = chunk * TILES + i
-            found[replica, row(tile)] = cut[:, :length]
-            found[replica, row(tiles + tile)] = cut[:, length:]
-        for part_x in range(2):
-            first = part_x * tiles + chunk * TILES
-            rows = pl.ds(side * first + (1 - side) * (rows_x - first - TILES), TILES)
-            copy = pltpu.make_async_copy(
-                found.at[replica, rows], out.at[replica, rows], sems_out.at[replica, chunk, part_x]
-            )
-            copy.start()
-            stores.append(copy)
+            out[replica, row(tile)] = cut[:, :length]
+            out[replica, row(tiles + tile)] = cut[:, length:]
 
     for replica in range(replicas):
         for chunk in range(chunks):
+            if replica == 1 and chunk == chunks - 1:
+                for copy in sends_zi.values():
+                    copy.wait_send()
             finish(replica, chunk)
-
-    for copy in [*sends_z.values(), *sends_y, *sends_c, *sends_ci, *sends_yi, *sends_zi.values()]:
-        copy.wait_send()
-    for copy in stores:
-        copy.wait()
 
 
 def twice(table):
@@ -453,12 +457,15 @@
     f32, bf16 = jnp.float32, jnp.bfloat16
     dma = pltpu.SemaphoreType.DMA
     sheet = (tiles, half, length)
-    given = (density, kernel_factors, *tables_of(length))
+    given = [
+        pltpu.with_memory_space_constraint(array, pltpu.HBM)
+        for array in (density, kernel_factors, *tables_of(length))
+    ]
     return pl.pallas_call(
         sector_kernel,
-        out_shape=jax.ShapeDtypeStruct(density.shape, f32),
+        out_shape=pltpu.VMEM(density.shape, f32),
         in_specs=[pl.BlockSpec(memory_space=pl.ANY)] * len(given),
-        out_specs=pl.BlockSpec(memory_space=pl.ANY),
+        out_specs=pl.BlockSpec(memory_space=pltpu.VMEM),
         scratch_shapes=[pltpu.VMEM(array.shape, array.dtype) for array in given] + [
             pltpu.VMEM((replicas, 2, tiles, rows_y, length), f32),
             pltpu.VMEM((tiles, length, length), f32),
@@ -470,12 +477,12 @@
             pltpu.VMEM((2,) + sheet, f32), pltpu.VMEM(sheet, f32),
             pltpu.VMEM((tiles, length, length), f32),
             pltpu.VMEM((replicas, 2, tiles, rows_y, length), f32),
-            pltpu.VMEM(density.shape, f32),
             pltpu.VMEM((3, length, length), f32), pltpu.VMEM((2, length, length), f32),
             pltpu.VMEM((2 * length, 2 * length), bf16),
+            pltpu.VMEM((GROUP, 2 * length, 2 * length), bf16),
             dma((2, count_py, chunks)), dma((2, chunks)), dma((2, chunks)),
             dma((2, chunks)), dma((2, chunks)), dma((2, count_py, chunks)),
-            dma((len(given) + 1,)), dma((replicas, chunks, 2)),
+            dma((len(given) + 1,)),
         ],
         compiler_params=pltpu.CompilerParams(
             has_side_effects=True, vmem_limit_bytes=56 * 2**20, collective_id=0

time: 73.5 us -> 67.5 us (0.918)
  Pallas kernels: 71 us -> 66.3 us
  local copies, waits for them, and re-layouts: 2.26 us -> 0.97 us
    pallas_call x1, Pallas kernels: 71 us -> 66.3 us  [sector_body(): pl.pallas_call(sector_kernel, out_shape=pltpu.VMEM(density.shape, f32), i...]
    unnamed x1, local copies, waits for them, and re-layouts: 2.26 us -> 0.97 us
where the time goes in v3:
time: 67.5 us; the launch traced here: 67.3 us
  Pallas kernels  66.3 us (98%)
  local copies, waits for them, and re-layouts  0.97 us (1%)
    pallas_call x1, Pallas kernels, sector_body(): pl.pallas_call(sector_kernel, out_shape=pltpu.VMEM(density.shape, f32), i...  66.3 us

profile of v3, /device:TPU:0, one launch (start us, length us, event | category | flops | bytes accessed | tf_op | source)
XLA Modules:
  0.0 67.3 jit_solution(7329326529164660198)
XLA Ops:
  0.0 66.3 %shard_map.100 = f32[2,32,32,128]{3,2,1,0:T(8,128)S(1)} custom-call(f32[2,32,32,128]{3,2,1,0:T(8,128)} %dens_in.1, f32[3,89,256]{2,1,0:T(8,128)} %factors_in.1, bf16[512,256]{1,0:T(8,128)(2,1)} %constant.16.clone.fold_z_in, bf16[128,256]{1,0:T(8,128)(2,1)} %constant.17.clone.fold_y_in, bf16[2,384,256]{2,1,0:T(8,128)(2,1)} %constant.18.clone.wide_in, ...), custom_call_target="tpu_custom_call" | custom-call | tf_op jit(solution)/shard_map/pallas_call | solution.py:464
  66.4 1.0 %copy.12 = f32[2,32,32,128]{3,2,1,0:T(8,128)} copy(f32[2,32,32,128]{3,2,1,0:T(8,128)S(1)} %shard_map.100) | data formatting | bytes 2097152

commit v4 on v3

v4 whole, which is shorter than its diff:
```python
import math

import jax
import jax.numpy as jnp
import numpy as np
from jax import lax
from jax.experimental import pallas as pl
from jax.experimental.pallas import tpu as pltpu
from jax.sharding import PartitionSpec as P

HIGHEST = lax.Precision.HIGHEST
LANES = 128
TILES = 2
LAG = 3
LAG_BACK = 3
GROUP = 8
PITCH = 129


def spectral_table(length, chunks):
    freq = np.arange(length).reshape(chunks, 1, length // chunks, 1)
    angle = (freq * np.arange(length) % (2 * length)) * (math.pi / length)
    both = np.concatenate([np.cos(angle), np.sin(angle)], 1)
    return both.reshape(2 * length, length).astype(np.float32)


def dot(spec, left, right):
    return jnp.einsum(spec, left, right, precision=HIGHEST, preferred_element_type=jnp.float32)


def kernel_block(factors, y_start, y_count, z_start, z_count):
    length = factors.shape[2] // 2
    weights = np.full((length,), 1.0 / length, np.float32)
    weights[0] = 0.5 / length
    factors = factors[:, :, :length] * weights
    factor_y = lax.dynamic_slice_in_dim(factors[1], y_start, y_count, 1)
    factor_z = lax.dynamic_slice_in_dim(factors[2], z_start, z_count, 1)
    pair = factor_z[:, :, None] * factor_y[:, None, :]
    return jnp.einsum("gzy,gx->zyx", pair, factors[0], precision=lax.Precision.HIGHEST)


def plain_body(density, kernel_factors):
    replicas, rows_x, rows_y, length = density.shape
    count_px = lax.axis_size("px")
    count_py = lax.axis_size("py")
    half = count_px // replicas
    trade = [[i + half * r for r in range(replicas)] for i in range(half)]
    lines = [[r * half + i for i in range(half)] for r in range(replicas)]
    index_x = lax.axis_index("px") % half
    index_y = lax.axis_index("py")
    table_z = spectral_table(length, count_py)
    table_y = spectral_table(length, half)
    order = np.arange(length).reshape(replicas, half, rows_x).transpose(1, 0, 2).reshape(-1)
    table_x = spectral_table(length, 1)[:, order]

    held = lax.all_to_all(density, "px", 0, 0, axis_index_groups=trade, tiled=True)
    held = held.reshape(replicas * rows_x, rows_y, length)
    held = dot("kz,xyz->kyx", table_z, held)
    held = lax.all_to_all(held, "py", 0, 1, tiled=True)
    held = dot("qy,kyx->kqx", table_y, held)
    held = lax.all_to_all(held, "px", 1, 2, axis_index_groups=lines, tiled=True)
    z_freq, y_freq = length // count_py, length // half
    kernel = kernel_block(kernel_factors, index_x * y_freq, y_freq, index_y * z_freq, z_freq)
    held = dot("kqx,px->kqp", held, table_x)
    held = held.reshape(2, z_freq, 2, y_freq, 2, length) * kernel[None, :, None, :, None, :]
    held = held.reshape(2 * z_freq, 2 * y_freq, 2 * length)
    held = dot("kqp,px->kqx", held, table_x)
    held = lax.all_to_all(held, "px", 2, 1, axis_index_groups=lines, tiled=True)
    held = dot("kqx,qy->kyx", held, table_y)
    held = lax.all_to_all(held, "py", 1, 0, tiled=True)
    held = dot("kyx,kz->xyz", held, table_z)
    held = held.reshape(replicas, rows_x, rows_y, length)
    return lax.all_to_all(held, "px", 0, 0, axis_index_groups=trade, tiled=True)


def halves(values):
    high = values.astype(jnp.bfloat16)
    low = (values - high.astype(jnp.float32)).astype(jnp.bfloat16)
    return high, low


def matmul(left, right):
    return lax.dot_general(left, right, (((1,), (0,)), ((), ())), preferred_element_type=jnp.float32)


def sector_kernel(
    dens_in, factors_in, tables_in, out,
    dens, factors, tables,
    a, z, b, p, swap, x, e, turned_e, kern, keep, c_send, c_held, g, g_send, zr, fin,
    flat, turned, gains, solved,
    sent, sems_z, sems_y, sems_c, sems_ci, sems_yi, sems_zi, sems_in,
):
    replicas, rows_x, rows_y, length = dens.shape
    half = length // 2
    tiles = rows_x // 2
    sizes = [TILES] * (tiles // TILES - 1) + [1] * TILES
    coming = [pl.ds(sum(sizes[:i]), size) for i, size in enumerate(sizes)]
    sizes = sizes[::-1]
    going = [pl.ds(sum(sizes[:i]), size) for i, size in enumerate(sizes)]
    chunks = len(sizes)
    me_px, me_py = lax.axis_index("px"), lax.axis_index("py")
    count_px, count_py = lax.axis_size("px"), lax.axis_size("py")
    side, core = lax.div(me_px, 2), lax.rem(me_px, 2)
    sign = 2 * side - 1
    part = side * (me_px - 2) + (1 - side) * (1 - me_px)
    peers = {1: me_py + 1 - 2 * lax.rem(me_py, 2), 2: lax.rem(me_py + 2, count_py), 3: count_py - 1 - me_py}

    def role(py):
        return lax.div(lax.rem(py + 1, count_py), 2), lax.div(py, 2)

    mine, odd_z = role(me_py)
    outer = mine == 0
    twin = count_px - 1 - me_px
    other = me_px + 1 - 2 * core

    barrier = pltpu.get_barrier_semaphore()
    partners = [{"py": peer} for peer in peers.values()] + [{"px": twin}, {"px": other}]
    for partner in partners:
        pl.semaphore_signal(barrier, inc=1, device_id=partner, device_id_type=pl.DeviceIdType.MESH)

    where_of, _ = layout_of(length)

    def table(name, parity=None):
        start, rows = where_of[name]
        if parity is None:
            return tables[start : start + rows, :]
        rows //= 2
        return tables[pl.ds(pl.multiple_of(start + parity * rows, 16), rows), :]

    loads = {}

    def load(name, src, dst):
        loads[name] = pltpu.make_async_copy(src, dst, sems_in.at[len(loads)])
        loads[name].start()

    early = pl.ds(0, where_of["fold_z"][1])
    late = pl.ds(early.size, tables.shape[0] - early.size)
    load("first", dens_in.at[0], dens.at[0])
    load("fold_z", tables_in.at[early], tables.at[early])
    load("rest", dens_in.at[pl.ds(1, replicas - 1)], dens.at[pl.ds(1, replicas - 1)])
    load("factors", factors_in, factors)
    load("tables", tables_in.at[late], tables.at[late])

    def make(src, dst, stage, sem, device):
        return pltpu.make_async_remote_copy(
            src_ref=src, dst_ref=dst, send_sem=sent.at[stage], recv_sem=sem,
            device_id=device, device_id_type=pl.DeviceIdType.MESH,
        )

    def arrived(ref, sem):
        make(ref, ref, 0, sem, {"px": other}).wait_recv()

    def gone(ref, stage):
        make(ref, ref, stage, sems_y.at[0], {"px": other}).wait_send()

    def lines(py):
        return pl.ds(pl.multiple_of(py * rows_y, 8), rows_y)

    three = pl.ds(0, (count_py - 1) * rows_y)

    def row(tile):
        return side * tile + (1 - side) * (rows_x - 1 - tile)

    def fold(replica, chunk):
        span = coming[chunk]
        left = [dens[replica, row(span.start + i)] for i in range(span.size)]
        right = [dens[replica, row(tiles + span.start + i)] for i in range(span.size)]
        both = jnp.concatenate([jnp.concatenate(left, 0), jnp.concatenate(right, 0)], 1)
        waves = matmul(jnp.concatenate(halves(both), 1), table("fold_z"))
        for parity in range(2):
            cut = waves[:, parity * length : (parity + 1) * length]
            a[replica, parity, span] = cut.reshape(span.size, rows_y, length)

    sends_z = {}
    for chunk in range(chunks):
        for step, peer in peers.items():
            replica, parity = role(peer)
            sends_z[step, chunk] = make(
                a.at[replica, parity, coming[chunk]], z.at[coming[chunk], lines(me_py), :],
                0, sems_z.at[chunk], {"py": peer},
            )

    def steps(replica):
        return ((3,), (2, 1)) if replica == 0 else ((2, 1), (3,))

    def scatter(replica, chunk):
        at_outer, at_inner = steps(replica)

        @pl.when(outer)
        def _():
            for step in at_outer:
                sends_z[step, chunk].start()

        @pl.when(jnp.logical_not(outer))
        def _():
            for step in at_inner:
                sends_z[step, chunk].start()

    loads["first"].wait()
    loads["fold_z"].wait()
    for replica in range(replicas):
        if replica == 1:
            loads["rest"].wait()
        for chunk in range(chunks):
            fold(replica, chunk)
            if replica == chunk == 0:
                pl.semaphore_wait(barrier, len(partners))
            scatter(replica, chunk)

    @pl.loop(0, tiles, unroll=4)
    def _(tile):
        z[tile, lines(me_py), :] = a[mine, odd_z, tile]

    def kernel_values():
        loads["factors"].wait()
        terms = factors.shape[1]
        flat[...] = jnp.zeros_like(flat)
        where = lax.broadcasted_iota(jnp.int32, (terms, length), 1)
        weight = jnp.where(where == 0, 0.5 / length, 1.0 / length)
        for dim in range(3):
            flat[dim, 0:terms] = factors[dim, :, 0:length] * weight
        for dim in range(2):
            turned[dim] = flat[dim].T
        high, low = halves(flat[2])
        gains[...] = jnp.concatenate(
            [jnp.concatenate([high, low], 1), jnp.concatenate([high, jnp.zeros_like(low)], 1)], 0
        )

        @pl.loop(0, length, unroll=8)
        def _(f):
            pair = turned[0] * turned[1, pl.ds(f, 1), :]
            sums = matmul(jnp.concatenate(halves(pair), 1), gains[...])
            kern[f] = sums[:, :length] + sums[:, length:]

    kernel_values()
    def fold_lines(chunk):
        span = coming[chunk]
        arrived(z.at[span, three, :], sems_z.at[chunk])
        for tile in range(span.start, span.start + span.size, 2):
            width = min(2, span.start + span.size - tile)
            cells = jnp.concatenate([z[tile + j] for j in range(width)], 1)
            waves = matmul(table("fold_y"), jnp.concatenate(halves(cells), 0))
            for parity in range(2):
                for j in range(width):
                    b[parity, tile + j] = waves[
                        parity * half : (parity + 1) * half, j * length : (j + 1) * length
                    ]
        make(b.at[1 - side, span], p.at[span], 1, sems_y.at[chunk], {"px": twin}).start()

    flip = sign.astype(jnp.float32)
    def fold_sheets(chunk):
        span = coming[chunk]
        arrived(p.at[span], sems_y.at[chunk])
        for tile in range(span.start, span.start + span.size):
            ours, theirs = b[side, tile], p[tile]
            total, gap = ours + theirs, (ours - theirs) * flip
            x[part, tile] = jnp.where(core == 0, total, gap)
            swap[tile] = jnp.where(core == 0, gap, total)
        make(swap.at[span], x.at[part, span], 2, sems_c.at[chunk], {"px": other}).start()

    def forward(start, count, wheres):
        cells = [x[where, pl.ds(start, count)].reshape(count * half, length) for where in wheres]
        high, low = halves(jnp.concatenate(cells, 0))
        waves = matmul(jnp.concatenate([high, low, high], 1), table("wide", odd_z))
        tall = table("tall", side)[:, : 3 * half]
        found = []
        for i in range(count * len(wheres)):
            high, low = halves(waves[i * half : (i + 1) * half])
            found.append(matmul(tall, jnp.concatenate([high, high, low], 0)))
        for k, where in enumerate(wheres):
            for i in range(count):
                for j in range(2):
                    first = (where * rows_x + j * tiles + start + i) * PITCH
                    e[pl.ds(first, length), :] = found[k * count + i][
                        :, j * length : (j + 1) * length
                    ]

    def forward_both(chunk, count):
        for one in range(chunk, chunk + count):
            arrived(swap.at[coming[one]], sems_c.at[one])
        tiles_here = sum(span.size for span in coming[chunk : chunk + count])
        forward(coming[chunk].start, tiles_here, (part, 1 - part))

    def forward_last():
        arrived(swap.at[coming[-1]], sems_c.at[chunks - 1])
        forward(coming[-1].start, coming[-1].size, (1 - part,))

    loads["tables"].wait()
    for stage in range(chunks + LAG + 1):
        if stage < chunks:
            fold_lines(stage)
        if 0 <= stage - LAG < chunks:
            fold_sheets(stage - LAG)
        if stage - LAG == chunks - 1:
            forward(coming[-1].start, coming[-1].size, (part,))
        ready = stage - LAG - 3
        if ready >= 0 and ready % 2 == 0:
            forward_both(ready, 2)
    forward_last()

    def spectrum(first):
        cells = jnp.concatenate([e[pl.ds(first + i, half, stride=PITCH), :] for i in range(2)], 1)
        high, low = halves(cells)
        return matmul(table("tall", core)[:, : 3 * half], jnp.concatenate([high, high, low], 0))

    def answer_of(first, k):
        cells = matmul(table("back_tall", core), solved[k])
        cells = cells[:half] + cells[half:]
        for i in range(2):
            turned_e[pl.ds(first + i, half, stride=PITCH), :] = cells[:, i * length : (i + 1) * length]

    def solve(first, k, waves):
        product = waves * jnp.concatenate([kern[first], kern[first + 1]], 1)
        solved[k] = jnp.concatenate(halves(product), 0)

    def middle():
        trips = length // (2 * GROUP)
        for k in range(GROUP):
            solve(2 * k, k, spectrum(2 * k))

        @pl.loop(1, trips)
        def _(f):
            for k in range(GROUP):
                first = 2 * (f * GROUP + k)
                waves = spectrum(first)
                answer_of(first - 2 * GROUP, k)
                solve(first, k, waves)

        for k in range(GROUP):
            answer_of(length - 2 * GROUP + 2 * k, k)

    middle()

    def backward(chunk):
        span = going[chunk]
        rows = []
        for where in (1 - part, part):
            for i in range(span.size):
                cells = []
                for j in range(2):
                    start = (where * rows_x + j * tiles + span.start + i) * PITCH
                    cells.append(turned_e[pl.ds(start, length), :])
                cells = jnp.concatenate(halves(jnp.concatenate(cells, 1)), 0)
                cells = matmul(table("back_tall", side), cells)
                rows.append(cells[:half] + cells[half:])
        high, low = halves(jnp.concatenate(rows, 0))
        wide = table("back_wide", odd_z)
        wide = jnp.concatenate([wide[:, :length], wide[:, length:]], 0)
        cells = matmul(jnp.concatenate([high, low, high], 1), wide)
        found = cells.reshape(2, span.size, half, length)
        c_send[span], keep[span] = found[0], found[1]
        make(c_send.at[span], c_held.at[span], 3, sems_ci.at[chunk], {"px": other}).start()

    def open_sheets(chunk):
        span = going[chunk]
        arrived(c_held.at[span], sems_ci.at[chunk])
        for tile in range(span.start, span.start + span.size):
            first, second = keep[tile], c_held[tile]
            even = jnp.where(core == 0, first, second)
            odd = jnp.where(core == 0, second, first) * flip
            g[side, tile] = even + odd
            g_send[tile] = even - odd
        make(g_send.at[span], g.at[side, span], 4, sems_yi.at[chunk], {"px": twin}).start()

    def answer(step, chunk):
        span = going[chunk]
        return make(
            zr.at[span, lines(peers[step]), :], fin.at[mine, odd_z, span],
            5, sems_zi.at[mine, chunk], {"py": peers[step]},
        )

    def open_lines(chunk):
        span = going[chunk]
        arrived(g_send.at[span], sems_yi.at[chunk])
        for tile in range(span.start, span.start + span.size, 2):
            width = min(2, span.start + span.size - tile)
            both = [
                jnp.concatenate([g[parity, tile + j] for j in range(width)], 1) for parity in range(2)
            ]
            cells = matmul(table("open_y"), jnp.concatenate(halves(jnp.concatenate(both, 0)), 0))
            for j in range(width):
                zr[tile + j] = cells[:, j * length : (j + 1) * length]
        for step in (3, 2):
            answer(step, chunk).start()

        @pl.when(jnp.logical_not(outer))
        def _():
            answer(1, chunk).start()

        fin[mine, odd_z, span] = zr[span, lines(me_py), :]

    for stage in range(chunks + LAG_BACK + 1):
        if stage < chunks:
            backward(stage)
        if 0 <= stage - 1 < chunks:
            open_sheets(stage - 1)
        if 0 <= stage - LAG_BACK - 1:
            open_lines(stage - LAG_BACK - 1)

    @pl.when(outer)
    def _():
        for chunk in range(chunks):
            answer(1, chunk).start()

    for stage, ref in enumerate((z.at[:, three, :], p, swap, c_send, g_send)):
        gone(ref, stage)

    def finish(replica, chunk):
        span = going[chunk]
        few, many = (outer, jnp.logical_not(outer))[:: 1 - 2 * replica]

        @pl.when(few)
        def _():
            arrived(fin.at[replica, 0, span], sems_zi.at[replica, chunk])

        @pl.when(many)
        def _():
            arrived(fin.at[replica, :, span], sems_zi.at[replica, chunk])

        both = [fin[replica, parity, span].reshape(span.size * rows_y, length) for parity in range(2)]
        cells = matmul(jnp.concatenate(halves(jnp.concatenate(both, 1)), 1), table("open_z"))
        for i in range(span.size):
            cut = cells[i * rows_y : (i + 1) * rows_y]
            out[replica, row(span.start + i)] = cut[:, :length]
            out[replica, row(tiles + span.start + i)] = cut[:, length:]

    for replica in range(replicas):
        for chunk in range(chunks):
            if replica == 1 and chunk == chunks - 1:
                gone(zr.at[:, three, :], 5)
            finish(replica, chunk)


def twice(table):
    zero = np.zeros_like(table)
    return np.block([[table, zero], [zero, table]])


def tables_of(length):
    half = length // 2
    angle = (np.arange(length)[:, None] * (2 * np.arange(half) + 1) % (4 * length)) * (math.pi / (2 * length))
    waves = np.stack([np.cos(angle), np.sin(angle)]).astype(np.float32)
    high = waves.astype(jnp.bfloat16).astype(np.float32)
    low = waves - high
    near, far = np.eye(half), np.eye(half)[::-1]
    line = np.block([[far, near], [-far, near]])
    sides = [line[:half].T, line[half:].T]
    fold_z = np.concatenate([twice(side) for side in sides], 1)
    fold_z = np.concatenate([fold_z, fold_z], 0)
    fold_y = np.concatenate([line, line], 1)
    open_y = np.concatenate([line.T, line.T], 1)
    open_z = np.concatenate([twice(side.T) for side in sides], 0)
    open_z = np.concatenate([open_z, open_z], 0)
    wide, tall, back_tall, back_wide = [], [], [], []
    for parity in range(2):
        up, down = high[parity], low[parity]
        wide.append(np.concatenate([twice(up.T), twice(up.T), twice(down.T)], 0))
        tall.append(np.concatenate([up, down, up], 1))
        back_tall.append(np.block([[up.T, up.T], [down.T, np.zeros_like(down.T)]]))
        back_wide.append(np.concatenate([twice(up), twice(up), twice(down)], 0))
    tall = np.concatenate(tall, 0)
    back_wide = [np.concatenate(np.split(one, 2, 0), 1) for one in back_wide]
    found = {
        "fold_z": fold_z, "fold_y": fold_y, "wide": np.concatenate(wide, 0),
        "tall": np.pad(tall, ((0, 0), (0, 2 * length - tall.shape[1]))),
        "back_tall": np.concatenate(back_tall, 0), "back_wide": np.concatenate(back_wide, 0),
        "open_y": open_y, "open_z": open_z,
    }
    return {name: one.astype(np.float32).astype(jnp.bfloat16) for name, one in found.items()}


def layout_of(length):
    found, start = {}, 0
    tables = tables_of(length)
    for name, one in tables.items():
        found[name] = (start, one.shape[0])
        start += one.shape[0]
    return found, np.concatenate(list(tables.values()), 0)


def sector_body(density, kernel_factors):
    replicas, rows_x, rows_y, length = density.shape
    half, tiles = length // 2, rows_x // 2
    chunks = tiles // TILES - 1 + TILES
    f32, bf16 = jnp.float32, jnp.bfloat16
    dma = pltpu.SemaphoreType.DMA
    sheet = (tiles, half, length)
    given = [
        pltpu.with_memory_space_constraint(array, pltpu.HBM)
        for array in (density, kernel_factors, jnp.asarray(layout_of(length)[1]))
    ]
    return pl.pallas_call(
        sector_kernel,
        out_shape=pltpu.VMEM(density.shape, f32),
        in_specs=[pl.BlockSpec(memory_space=pl.ANY)] * len(given),
        out_specs=pl.BlockSpec(memory_space=pltpu.VMEM),
        scratch_shapes=[pltpu.VMEM(array.shape, array.dtype) for array in given] + [
            pltpu.VMEM((replicas, 2, tiles, rows_y, length), f32),
            pltpu.VMEM((tiles, length, length), f32),
            pltpu.VMEM((2,) + sheet, f32), pltpu.VMEM(sheet, f32), pltpu.VMEM(sheet, f32),
            pltpu.VMEM((2,) + sheet, f32),
            pltpu.VMEM((half * PITCH, length), f32), pltpu.VMEM((half * PITCH, length), f32),
            pltpu.VMEM((length, length, length), f32),
            pltpu.VMEM(sheet, f32), pltpu.VMEM(sheet, f32), pltpu.VMEM(sheet, f32),
            pltpu.VMEM((2,) + sheet, f32), pltpu.VMEM(sheet, f32),
            pltpu.VMEM((tiles, length, length), f32),
            pltpu.VMEM((replicas, 2, tiles, rows_y, length), f32),
            pltpu.VMEM((3, length, length), f32), pltpu.VMEM((2, length, length), f32),
            pltpu.VMEM((2 * length, 2 * length), bf16),
            pltpu.VMEM((GROUP, 2 * length, 2 * length), bf16),
            dma((6,)), dma((chunks,)), dma((chunks,)), dma((chunks,)),
            dma((chunks,)), dma((chunks,)), dma((replicas, chunks)), dma((5,)),
        ],
        compiler_params=pltpu.CompilerParams(
            has_side_effects=True, vmem_limit_bytes=56 * 2**20, collective_id=0
        ),
    )(*given)


def body(density, kernel_factors):
    replicas, rows_x, rows_y, length = density.shape
    count_px, count_py = lax.axis_size("px"), lax.axis_size("py")
    square = count_px == count_py == 2 * replicas == 4
    whole = rows_x * count_px == rows_y * count_py == length == LANES
    if square and whole and kernel_factors.shape[1] <= LANES:
        return sector_body(density, kernel_factors)
    return plain_body(density, kernel_factors)


def solution(mesh):
    placed = (P("rep", "px", "py", None), P())
    return jax.shard_map(
        body, mesh=mesh, in_specs=placed, out_specs=P("rep", "px", "py", None), check_vma=False
    )
```

time: 67.5 us -> 66.1 us (0.979)
  Pallas kernels: 66.3 us -> 64.9 us
    pallas_call x1, Pallas kernels: 66.3 us -> 64.9 us  [sector_body(): pl.pallas_call(sector_kernel, out_shape=pltpu.VMEM(density.shape, f32), i...]
where the time goes in v4:
time: 66.1 us; the launch traced here: 65.9 us
  Pallas kernels  64.9 us (98%)
  local copies, waits for them, and re-layouts  0.97 us (1%)
    pallas_call x1, Pallas kernels, sector_body(): pl.pallas_call(sector_kernel, out_shape=pltpu.VMEM(density.shape, f32), i...  64.9 us

profile of v4, /device:TPU:0, one launch (start us, length us, event | category | flops | bytes accessed | tf_op | source)
XLA Modules:
  0.0 65.9 jit_solution(4334917507688569108)
XLA Ops:
  0.0 64.9 %shard_map.37 = f32[2,32,32,128]{3,2,1,0:T(8,128)S(1)} custom-call(f32[2,32,32,128]{3,2,1,0:T(8,128)} %dens_in.1, f32[3,89,256]{2,1,0:T(8,128)} %factors_in.1, bf16[3328,256]{1,0:T(8,128)(2,1)} %constant.2.clone.tables_in), custom_call_target="tpu_custom_call" | custom-call | tf_op jit(solution)/shard_map/pallas_call | solution.py:492
  64.9 1.0 %copy.5 = f32[2,32,32,128]{3,2,1,0:T(8,128)} copy(f32[2,32,32,128]{3,2,1,0:T(8,128)S(1)} %shard_map.37) | data formatting | bytes 2097152

commit v5 on v4

--- a/solution.py
+++ b/solution.py
@@ -11,7 +11,7 @@
 HIGHEST = lax.Precision.HIGHEST
 LANES = 128
 TILES = 2
-LAG = 3
+LAG = 4
 LAG_BACK = 3
 GROUP = 8
 PITCH = 129
@@ -93,9 +93,8 @@
     replicas, rows_x, rows_y, length = dens.shape
     half = length // 2
     tiles = rows_x // 2
-    sizes = [TILES] * (tiles // TILES - 1) + [1] * TILES
+    sizes = [1] * TILES + [TILES] * (tiles // TILES - 2) + [1] * TILES
     coming = [pl.ds(sum(sizes[:i]), size) for i, size in enumerate(sizes)]
-    sizes = sizes[::-1]
     going = [pl.ds(sum(sizes[:i]), size) for i, size in enumerate(sizes)]
     chunks = len(sizes)
     me_px, me_py = lax.axis_index("px"), lax.axis_index("py")
@@ -211,7 +210,7 @@
     def _(tile):
         z[tile, lines(me_py), :] = a[mine, odd_z, tile]
 
-    def kernel_values():
+    def kernel_setup():
         loads["factors"].wait()
         terms = factors.shape[1]
         flat[...] = jnp.zeros_like(flat)
@@ -226,13 +225,16 @@
             [jnp.concatenate([high, low], 1), jnp.concatenate([high, jnp.zeros_like(low)], 1)], 0
         )
 
-        @pl.loop(0, length, unroll=8)
+    def kernel_values(start, count):
+        @pl.loop(start, start + count, unroll=8)
         def _(f):
             pair = turned[0] * turned[1, pl.ds(f, 1), :]
             sums = matmul(jnp.concatenate(halves(pair), 1), gains[...])
             kern[f] = sums[:, :length] + sums[:, length:]
 
-    kernel_values()
+    kernel_setup()
+    kernel_values(0, half)
+
     def fold_lines(chunk):
         span = coming[chunk]
         arrived(z.at[span, three, :], sems_z.at[chunk])
@@ -258,45 +260,44 @@
             swap[tile] = jnp.where(core == 0, gap, total)
         make(swap.at[span], x.at[part, span], 2, sems_c.at[chunk], {"px": other}).start()
 
-    def forward(start, count, wheres):
-        cells = [x[where, pl.ds(start, count)].reshape(count * half, length) for where in wheres]
+    def forward(pieces):
+        cells = [x[where, span].reshape(span.size * half, length) for where, span in pieces]
         high, low = halves(jnp.concatenate(cells, 0))
         waves = matmul(jnp.concatenate([high, low, high], 1), table("wide", odd_z))
         tall = table("tall", side)[:, : 3 * half]
+        each = [(where, tile) for where, span in pieces for tile in range(span.start, span.start + span.size)]
         found = []
-        for i in range(count * len(wheres)):
+        for i in range(len(each)):
             high, low = halves(waves[i * half : (i + 1) * half])
             found.append(matmul(tall, jnp.concatenate([high, high, low], 0)))
-        for k, where in enumerate(wheres):
-            for i in range(count):
-                for j in range(2):
-                    first = (where * rows_x + j * tiles + start + i) * PITCH
-                    e[pl.ds(first, length), :] = found[k * count + i][
-                        :, j * length : (j + 1) * length
-                    ]
-
-    def forward_both(chunk, count):
-        for one in range(chunk, chunk + count):
-            arrived(swap.at[coming[one]], sems_c.at[one])
-        tiles_here = sum(span.size for span in coming[chunk : chunk + count])
-        forward(coming[chunk].start, tiles_here, (part, 1 - part))
-
-    def forward_last():
-        arrived(swap.at[coming[-1]], sems_c.at[chunks - 1])
-        forward(coming[-1].start, coming[-1].size, (1 - part,))
+        for both, (where, tile) in zip(found, each):
+            for j in range(2):
+                first = (where * rows_x + j * tiles + tile) * PITCH
+                e[pl.ds(first, length), :] = both[:, j * length : (j + 1) * length]
+
+    def swapped(chunk):
+        arrived(swap.at[coming[chunk]], sems_c.at[chunk])
 
     loads["tables"].wait()
-    for stage in range(chunks + LAG + 1):
+    for stage in range(chunks + LAG):
         if stage < chunks:
             fold_lines(stage)
-        if 0 <= stage - LAG < chunks:
+        if stage < 4:
+            kernel_values(half + stage * half // 4, half // 4)
+        if stage >= LAG:
             fold_sheets(stage - LAG)
-        if stage - LAG == chunks - 1:
-            forward(coming[-1].start, coming[-1].size, (part,))
         ready = stage - LAG - 3
-        if ready >= 0 and ready % 2 == 0:
-            forward_both(ready, 2)
-    forward_last()
+        if ready >= 0 and ready % 2 == 0 and ready < chunks - 4:
+            some = coming[ready : ready + 2]
+            swapped(ready)
+            swapped(ready + 1)
+            forward([(where, span) for where in (part, 1 - part) for span in some])
+    forward([(part, span) for span in coming[-4:]])
+    for chunk in range(chunks - 4, chunks - 1):
+        swapped(chunk)
+    forward([(1 - part, span) for span in coming[-4:-1]])
+    swapped(chunks - 1)
+    forward([(1 - part, coming[-1])])
 
     def spectrum(first):
         cells = jnp.concatenate([e[pl.ds(first + i, half, stride=PITCH), :] for i in range(2)], 1)
@@ -481,7 +482,7 @@
 def sector_body(density, kernel_factors):
     replicas, rows_x, rows_y, length = density.shape
     half, tiles = length // 2, rows_x // 2
-    chunks = tiles // TILES - 1 + TILES
+    chunks = tiles // TILES - 2 + 2 * TILES
     f32, bf16 = jnp.float32, jnp.bfloat16
     dma = pltpu.SemaphoreType.DMA
     sheet = (tiles, half, length)

time: 66.1 us -> 65.4 us (0.989)
  Pallas kernels: 64.9 us -> 64.2 us
    pallas_call x1, Pallas kernels: 64.9 us -> 64.2 us  [sector_body(): pl.pallas_call(sector_kernel, out_shape=pltpu.VMEM(density.shape, f32), i...]
where the time goes in v5:
time: 65.4 us; the launch traced here: 65.2 us
  Pallas kernels  64.2 us (98%)
  local copies, waits for them, and re-layouts  0.97 us (1%)
    pallas_call x1, Pallas kernels, sector_body(): pl.pallas_call(sector_kernel, out_shape=pltpu.VMEM(density.shape, f32), i...  64.2 us

profile of v5, /device:TPU:0, one launch (start us, length us, event | category | flops | bytes accessed | tf_op | source)
XLA Modules:
  0.0 65.2 jit_solution(4747202560968871846)
XLA Ops:
  0.0 64.2 %shard_map.37 = f32[2,32,32,128]{3,2,1,0:T(8,128)S(1)} custom-call(f32[2,32,32,128]{3,2,1,0:T(8,128)} %dens_in.1, f32[3,89,256]{2,1,0:T(8,128)} %factors_in.1, bf16[3328,256]{1,0:T(8,128)(2,1)} %constant.2.clone.tables_in), custom_call_target="tpu_custom_call" | custom-call | tf_op jit(solution)/shard_map/pallas_call | solution.py:493
  64.3 1.0 %copy.5 = f32[2,32,32,128]{3,2,1,0:T(8,128)} copy(f32[2,32,32,128]{3,2,1,0:T(8,128)S(1)} %shard_map.37) | data formatting | bytes 2097152

commit v6 on v5

--- a/solution.py
+++ b/solution.py
@@ -13,7 +13,7 @@
 TILES = 2
 LAG = 4
 LAG_BACK = 3
-GROUP = 8
+GROUP = 16
 PITCH = 129
 
 
@@ -109,6 +109,7 @@
 
     mine, odd_z = role(me_py)
     outer = mine == 0
+    inner = jnp.logical_not(outer)
     twin = count_px - 1 - me_px
     other = me_px + 1 - 2 * core
 
@@ -367,7 +368,7 @@
         span = going[chunk]
         return make(
             zr.at[span, lines(peers[step]), :], fin.at[mine, odd_z, span],
-            5, sems_zi.at[mine, chunk], {"py": peers[step]},
+            5, sems_zi.at[mine * (chunk + 1)], {"py": peers[step]},
         )
 
     def open_lines(chunk):
@@ -406,18 +407,21 @@
     for stage, ref in enumerate((z.at[:, three, :], p, swap, c_send, g_send)):
         gone(ref, stage)
 
+    def collect(replica, span, sem):
+        few, many = (outer, inner)[:: 1 - 2 * replica]
+
+        @pl.when(few)
+        def _():
+            arrived(fin.at[replica, 0, span], sem)
+
+        @pl.when(many)
+        def _():
+            arrived(fin.at[replica, :, span], sem)
+
     def finish(replica, chunk):
         span = going[chunk]
-        few, many = (outer, jnp.logical_not(outer))[:: 1 - 2 * replica]
-
-        @pl.when(few)
-        def _():
-            arrived(fin.at[replica, 0, span], sems_zi.at[replica, chunk])
-
-        @pl.when(many)
-        def _():
-            arrived(fin.at[replica, :, span], sems_zi.at[replica, chunk])
-
+        if replica == 1:
+            collect(replica, span, sems_zi.at[chunk + 1])
         both = [fin[replica, parity, span].reshape(span.size * rows_y, length) for parity in range(2)]
         cells = matmul(jnp.concatenate(halves(jnp.concatenate(both, 1)), 1), table("open_z"))
         for i in range(span.size):
@@ -425,6 +429,7 @@
             out[replica, row(span.start + i)] = cut[:, :length]
             out[replica, row(tiles + span.start + i)] = cut[:, length:]
 
+    collect(0, pl.ds(0, tiles), sems_zi.at[0])
     for replica in range(replicas):
         for chunk in range(chunks):
             if replica == 1 and chunk == chunks - 1:
@@ -510,7 +515,7 @@
             pltpu.VMEM((2 * length, 2 * length), bf16),
             pltpu.VMEM((GROUP, 2 * length, 2 * length), bf16),
             dma((6,)), dma((chunks,)), dma((chunks,)), dma((chunks,)),
-            dma((chunks,)), dma((chunks,)), dma((replicas, chunks)), dma((5,)),
+            dma((chunks,)), dma((chunks,)), dma((chunks + 1,)), dma((5,)),
         ],
         compiler_params=pltpu.CompilerParams(
             has_side_effects=True, vmem_limit_bytes=56 * 2**20, collective_id=0

time: 65.4 us -> 64.6 us (0.988)
  Pallas kernels: 64.2 us -> 63.5 us
    pallas_call x1, Pallas kernels: 64.2 us -> 63.5 us  [sector_body(): pl.pallas_call(sector_kernel, out_shape=pltpu.VMEM(density.shape, f32), i...]
where the time goes in v6:
time: 64.6 us; the launch traced here: 64.5 us
  Pallas kernels  63.5 us (98%)
  local copies, waits for them, and re-layouts  0.97 us (2%)
    pallas_call x1, Pallas kernels, sector_body(): pl.pallas_call(sector_kernel, out_shape=pltpu.VMEM(density.shape, f32), i...  63.5 us

profile of v6, /device:TPU:0, one launch (start us, length us, event | category | flops | bytes accessed | tf_op | source)
XLA Modules:
  0.0 64.5 jit_solution(6283702431320992664)
XLA Ops:
  0.0 63.5 %shard_map.37 = f32[2,32,32,128]{3,2,1,0:T(8,128)S(1)} custom-call(f32[2,32,32,128]{3,2,1,0:T(8,128)} %dens_in.1, f32[3,89,256]{2,1,0:T(8,128)} %factors_in.1, bf16[3328,256]{1,0:T(8,128)(2,1)} %constant.2.clone.tables_in), custom_call_target="tpu_custom_call" | custom-call | tf_op jit(solution)/shard_map/pallas_call | solution.py:498
  63.5 1.0 %copy.5 = f32[2,32,32,128]{3,2,1,0:T(8,128)} copy(f32[2,32,32,128]{3,2,1,0:T(8,128)S(1)} %shard_map.37) | data formatting | bytes 2097152

commit v7 on v6

--- a/solution.py
+++ b/solution.py
@@ -13,7 +13,7 @@
 TILES = 2
 LAG = 4
 LAG_BACK = 3
-GROUP = 16
+GROUP = 32
 PITCH = 129
 
 

time: 64.6 us -> 64.4 us (level)
  no operation moved by 1% of the time
where the time goes in v7:
time: 64.4 us; the launch traced here: 64.2 us
  Pallas kernels  63.3 us (98%)
  local copies, waits for them, and re-layouts  0.97 us (2%)
    pallas_call x1, Pallas kernels, sector_body(): pl.pallas_call(sector_kernel, out_shape=pltpu.VMEM(density.shape, f32), i...  63.3 us

profile of v7, /device:TPU:0, one launch (start us, length us, event | category | flops | bytes accessed | tf_op | source)
XLA Modules:
  0.0 64.2 jit_solution(11006487598982331165)
XLA Ops:
  0.0 63.3 %shard_map.37 = f32[2,32,32,128]{3,2,1,0:T(8,128)S(1)} custom-call(f32[2,32,32,128]{3,2,1,0:T(8,128)} %dens_in.1, f32[3,89,256]{2,1,0:T(8,128)} %factors_in.1, bf16[3328,256]{1,0:T(8,128)(2,1)} %constant.2.clone.tables_in), custom_call_target="tpu_custom_call" | custom-call | tf_op jit(solution)/shard_map/pallas_call | solution.py:498
  63.3 1.0 %copy.5 = f32[2,32,32,128]{3,2,1,0:T(8,128)} copy(f32[2,32,32,128]{3,2,1,0:T(8,128)S(1)} %shard_map.37) | data formatting | bytes 2097152
